TPU v7x, 128 devices: a whole 4x4x4 slice. The times are simulated.
128 devices in a mesh: section: 2 (over y_lo), row: 4 (over y_hi, core), col: 16 (over x, z).
Axes of the slice: x: 4, y: 4 (y_hi: 2, y_lo: 2; y = y_hi * 2 + y_lo), z: 4, core: 2. Of those that a mesh axis runs over, the one named last changes fastest.
Arguments:
- stash_inputs: bfloat16 [2, 4, 512, 12288], P('section', None, 'row', 'col'), may hold values from -16 to 16
- stash_hidden: bfloat16 [2, 4, 512, 24576], P('section', None, 'col', 'row'), may hold values from -6 to 6
- grad_in: bfloat16 [2, 512, 12288], P('section', 'row', 'col'), may hold values from -6 to 6
- w_in: bfloat16 [2, 12288, 24576], P('section', 'col', 'row'), may hold values from -0.0546875 to 0.0546875
- b_in: float32 [2, 24576], P('section', 'row'), may hold values from -3 to 3
- w_out: bfloat16 [2, 24576, 12288], P('section', 'row', 'col'), may hold values from -0.0390625 to 0.0390625
- b_out: float32 [2, 12288], P('section', 'col'), may hold values from -3 to 3
- ln_gain: float32 [2, 12288], P('section', 'col'), may hold values from 0.4 to 1.6
- plan: int32 [2, 2], P('section'), may hold values from 0 to 3, as said below
Outputs:
- act_recv: bfloat16 [2, 512, 12288], P('section', 'row', 'col')
- grad_recv: bfloat16 [2, 512, 12288], P('section', 'row', 'col')
- saved_hidden: bfloat16 [2, 512, 24576], P('section', 'col', 'row')
Inputs may be any that keep to these rules, and one draw needn't show every extreme that they name: plan[s, 0] is the stash slot of the micro-batch that section s takes backward, plan[s, 1] that of the one it takes forward; the two differ.
All inputs are finite; a program needn't handle non-finite values.
Results may differ from a plain program's by a relative error of at most 0.015.
Values may be sent and summed in bfloat16 or wider, within the bound.
A program may use at most 128 MiB of HBM per device.

v0:
```python
import jax
import jax.numpy as jnp
from jax import lax
from jax.sharding import PartitionSpec as P

D = 12288


epsilon = 1e-05
root_coef = 0.7978845608028654
cubic_coef = 0.044715


def copy_for_each(array, axis):
    copies = jnp.broadcast_to(array, (lax.axis_size(axis), *array.shape))
    return lax.all_to_all(copies, axis, split_axis=0, concat_axis=0, tiled=True)


def of_everyone(array, axis):
    return copy_for_each(array, axis).sum(axis=0)


def in_one(arrays, axis):
    ends = [0]
    for a in arrays:
        ends.append(ends[-1] + a.size)
    total = of_everyone(jnp.concatenate([a.ravel() for a in arrays]), axis)
    return tuple((total[b:e].reshape(a.shape) for a, b, e in zip(arrays, ends, ends[1:])))


def shifted(array, axis, by):
    size = lax.axis_size(axis)
    return lax.ppermute(array, axis, [(i, (i + by) % size) for i in range(size)])


def gelu_value(values):
    inner = root_coef * (values + cubic_coef * values * values * values)
    return 0.5 * values * (1.0 + jnp.tanh(inner))


def gelu_slope(values):
    inner = root_coef * (values + cubic_coef * values * values * values)
    tangent = jnp.tanh(inner)
    return 0.5 * (1.0 + tangent) + 0.5 * values * (1.0 - tangent * tangent) * root_coef * (
        1.0 + 3.0 * cubic_coef * values * values
    )


def finish_norm(values, total, squares):
    mean_val = total / D
    sq_mean = squares / D
    inv_std = lax.rsqrt(sq_mean - mean_val * mean_val + epsilon)
    return ((values - mean_val[:, None]) * inv_std[:, None], inv_std)


def transposed(left, right):
    return lax.dot_general(
        left, right, (((1,), (1,)), ((), ())), preferred_element_type=jnp.float32
    )


def body(stash_inputs, stash_hidden, grad_in, w_in, b_in, w_out, b_out, ln_gain, plan):
    bwd_slot = plan[0, 0]
    fwd_slot = plan[0, 1]
    fwd_input = lax.dynamic_index_in_dim(stash_inputs[0], fwd_slot, 0, keepdims=False).astype(
        jnp.float32
    )
    bwd_input = lax.dynamic_index_in_dim(stash_inputs[0], bwd_slot, 0, keepdims=False).astype(
        jnp.float32
    )
    bwd_hidden = lax.dynamic_index_in_dim(stash_hidden[0], bwd_slot, 0, keepdims=False).astype(
        jnp.float32
    )
    upstream = grad_in[0]
    w_first = w_in[0]
    b_first = b_in[0]
    w_second = w_out[0]
    b_second = b_out[0]
    gain_part = ln_gain[0]
    feat_part = w_second.shape[1]
    hid_part = w_first.shape[1]
    sums = in_one(
        (
            jnp.sum(fwd_input, axis=1),
            jnp.sum(fwd_input * fwd_input, axis=1),
            jnp.sum(bwd_input, axis=1),
            jnp.sum(bwd_input * bwd_input, axis=1),
        ),
        "col",
    )
    fwd_hat, fwd_inv = finish_norm(fwd_input, sums[0], sums[1])
    bwd_hat, bwd_inv = finish_norm(bwd_input, sums[2], sums[3])
    normed = (fwd_hat * gain_part).astype(jnp.bfloat16)
    normed_all, upstream_all = (
        lax.all_gather(normed, "row", axis=0, tiled=True),
        lax.all_gather(upstream, "row", axis=0, tiled=True),
    )
    joint = lax.psum_scatter(
        jnp.concatenate(
            [
                jnp.dot(normed_all, w_first, preferred_element_type=jnp.float32),
                transposed(upstream_all, w_second),
            ],
            axis=1,
        ),
        "col",
        scatter_dimension=0,
        tiled=True,
    )
    hidden_pre = joint[:, :hid_part]
    slopes = joint[:, hid_part:]
    hidden = hidden_pre + b_first
    saved = hidden.astype(jnp.bfloat16)
    activated = gelu_value(hidden).astype(jnp.bfloat16)
    hid_grad = (slopes * gelu_slope(bwd_hidden)).astype(jnp.bfloat16)
    paired = jnp.stack([activated, hid_grad], axis=1)
    piece = lax.all_gather(paired, "col", axis=0, tiled=True)
    terms = jnp.concatenate(
        [
            jnp.dot(piece[:, 0], w_second, preferred_element_type=jnp.float32),
            transposed(piece[:, 1], w_first),
        ],
        axis=1,
    )
    joint_out = lax.psum_scatter(terms, "row", scatter_dimension=0, tiled=True)
    out_sum = joint_out[:, :feat_part]
    norm_grad = joint_out[:, feat_part:]
    output = (out_sum + b_second + fwd_input).astype(jnp.bfloat16)
    scaled = norm_grad * gain_part
    grad_sums = in_one((jnp.sum(scaled, axis=1), jnp.sum(scaled * bwd_hat, axis=1)), "col")
    first_mean = grad_sums[0] / D
    second_mean = grad_sums[1] / D
    in_grad = upstream.astype(jnp.float32) + bwd_inv[:, None] * (
        scaled - first_mean[:, None] - bwd_hat * second_mean[:, None]
    )
    act_recv = shifted(output, "section", 1)
    grad_recv = shifted(in_grad.astype(jnp.bfloat16), "section", -1)
    return (act_recv[None], grad_recv[None], saved[None])


def solution(mesh):
    in_specs = (
        P("section", None, "row", "col"),
        P("section", None, "col", "row"),
        P("section", "row", "col"),
        P("section", "col", "row"),
        P("section", "row"),
        P("section", "row", "col"),
        P("section", "col"),
        P("section", "col"),
        P("section", None),
    )
    out_specs = (P("section", "row", "col"), P("section", "row", "col"), P("section", "col", "row"))
    return jax.shard_map(body, mesh=mesh, in_specs=in_specs, out_specs=out_specs, check_vma=False)
```

profile of v0, /device:TPU:1, one launch (start us, length us, event | category | flops | bytes accessed | tf_op | source)
XLA Modules:
  0.0 418.7 jit_solution(16272810926541566935)
XLA Ops:
  7.2 1.3 fusion.47
  12.4 1.2 convert_reduce_fusion.1
  13.5 1.2 fusion.29
  14.7 0.6 broadcast_in_dim.10
  15.4 8.4 %all-to-all-start = ((f32[16,1,512]{2,1,0:T(1,128)}), f32[16,1,512]{2,1,0:T(1,128)S(1)}, u32[]{:S(2)}, u32[]{:S(2)}) async-start(f32[16,1,512]{2,1,0:T(1,128)} %broadcast_in_dim.10), calls=%async_computation | async-start | bytes 65536 | tf_op jit(solution)/shard_map/all_to_all | solution.py:16
  23.8 0.0 reduce-scatter.3.cloned.1.call-start
  23.8 11.3 %all-gather = bf16[1,512,768]{2,1,0:T(8,128)(2,1)S(1)} all-gather(bf16[1,128,768]{2,1,0:T(8,128)(2,1)} %param.11), channel_id=2, replica_groups=mesh['section'=2,'row'=4,'col'=16] {'row'}, dimensions={1}, use_global_device_ids=true | all-gather | bytes 983040 | tf_op jit(solution)/shard_map/all_gather | solution.py:96
  35.1 11.7 %fusion.2 = f32[512,6144]{1,0:T(8,128)} fusion(bf16[1,6144,768]{2,1,0:T(8,128)(2,1)} %param.14, bf16[1,512,768]{2,1,0:T(8,128)(2,1)S(1)} %all-gather), kind=kOutput, calls=%fused_computation.3 | convolution fusion | flops 4831838208 | bytes 22806528 | tf_op jit(solution)/shard_map/dot_general | solution.py:57
  46.9 0.0 copy-done.3
  46.9 0.0 all-to-all-done
  46.9 0.0 copy-done
  47.0 0.1 fusion.32
  47.1 0.0 slice-start
  47.1 10.3 %all_gather.9 = bf16[512,768]{1,0:T(8,128)(2,1)S(1)} all-gather(bf16[128,768]{1,0:T(8,128)(2,1)S(1)} %fusion.32), channel_id=1, replica_groups=mesh['section'=2,'row'=4,'col'=16] {'row'}, dimensions={0}, use_global_device_ids=true | all-gather | bytes 983040 | tf_op jit(solution)/shard_map/all_gather | solution.py:95
  57.5 7.8 %fusion.6 = f32[512,6144]{1,0:T(8,128)S(1)} fusion(bf16[512,768]{1,0:T(8,128)(2,1)S(1)} %all_gather.9, bf16[1,768,6144]{2,1,0:T(8,128)(2,1)} %param.12), kind=kOutput, calls=%fused_computation.7 | convolution fusion | flops 4831838208 | bytes 22806528 | tf_op jit(solution)/shard_map/dot_general | solution.py:101
  65.3 0.0 slice-done
  65.3 0.0 slice-done.1
  65.3 0.0 slice-done.2
  65.3 8.6 %pad_maximum_fusion = f32[512,12288]{1,0:T(8,128)} fusion(f32[512,6144]{1,0:T(8,128)S(1)} %bitcast.82, f32[512,6144]{1,0:T(8,128)S(1)} %fusion.6), kind=kLoop, calls=%fused_computation | loop fusion | flops 6291456 | bytes 50331648 | tf_op jit(solution)/shard_map/concatenate | solution.py:99
  73.9 0.0 reduce-scatter.3.cloned.1.call-update
  74.0 0.0 all-gather.3.cloned.1.call-start
  74.0 153.3 %reduce-scatter.3.cloned.1.call-done = f32[32,12288]{1,0:T(8,128)} async-done(((f32[512,12288]{1,0:T(8,128)}), f32[32,12288]{1,0:T(8,128)}) %reduce-scatter.3.cloned.1.call-update) | async-done | bytes 1572880 | tf_op jit(solution)/shard_map/reduce_scatter | solution.py:98
  227.4 0.0 copy-done.2
  227.4 3.0 fusion.43
  230.4 1.0 pad_maximum_fusion.2
  231.3 0.0 all-gather.3.cloned.1.call-update
  231.4 0.0 reduce-scatter.5.cloned.1.call-start
  231.4 89.5 %all-gather.3.cloned.1.call-done = bf16[512,2,6144]{2,0,1:T(8,128)(2,1)} async-done(((bf16[32,2,6144]{2,0,1:T(8,128)(2,1)}), bf16[512,2,6144]{2,0,1:T(8,128)(2,1)}) %all-gather.3.cloned.1.call-update) | async-done | bytes 12582928 | tf_op jit(solution)/shard_map/all_gather | solution.py:117
  320.9 10.8 %fusion = f32[512,768]{1,0:T(8,128)S(1)} fusion(bf16[1,6144,768]{2,1,0:T(8,128)(2,1)} %param.14, bf16[512,2,6144]{2,0,1:T(8,128)(2,1)} %all-gather.3.cloned.1.call-done), kind=kOutput, calls=%fused_computation.1 | convolution fusion | flops 4831838208 | bytes 17301504 | tf_op jit(solution)/shard_map/dot_general | solution.py:120
  331.7 0.0 copy-done.5
  331.7 7.6 %fusion.4 = f32[512,768]{1,0:T(8,128)S(1)} fusion(bf16[1,768,6144]{2,1,0:T(8,128)(2,1)} %param.12, bf16[512,2,6144]{2,0,1:T(8,128)(2,1)S(1)} %copy-done.5), kind=kOutput, calls=%fused_computation.5 | convolution fusion | flops 4831838208 | bytes 17301504 | tf_op jit(solution)/shard_map/dot_general | solution.py:57
  339.3 0.0 copy-start.4
  339.3 0.0 copy-start.1
  339.3 2.0 pad_maximum_fusion.1
  341.4 0.0 reduce-scatter.5.cloned.1.call-update
  341.4 44.5 %reduce-scatter.5.cloned.1.call-done = f32[128,1536]{1,0:T(8,128)} async-done(((f32[512,1536]{1,0:T(8,128)}), f32[128,1536]{1,0:T(8,128)}) %reduce-scatter.5.cloned.1.call-update) | async-done | bytes 786448 | tf_op jit(solution)/shard_map/reduce_scatter | solution.py:125
  386.0 1.2 fusion.46
  387.2 0.6 broadcast_in_dim.24
  387.8 6.7 %all-to-all-start.1 = ((f32[16,1,256]{2,1,0:T(1,128)}), f32[16,1,256]{2,1,0:T(1,128)S(1)}, u32[]{:S(2)}, u32[]{:S(2)}) async-start(f32[16,1,256]{2,1,0:T(1,128)} %broadcast_in_dim.24), calls=%async_computation.3 | async-start | bytes 32768 | tf_op jit(solution)/shard_map/all_to_all | solution.py:16
  394.5 0.0 copy-done.4
  394.5 6.4 %all-to-all-done.1 = f32[16,1,256]{2,1,0:T(1,128)S(1)} async-done(((f32[16,1,256]{2,1,0:T(1,128)}), f32[16,1,256]{2,1,0:T(1,128)S(1)}, u32[]{:S(2)}, u32[]{:S(2)}) %all-to-all-start.1) | async-done | bytes 16416 | tf_op jit(solution)/shard_map/all_to_all | solution.py:16
  401.0 1.4 fusion.42
  402.3 0.4 collective-permute-start
  402.7 1.2 collective-permute-start.1
  403.9 3.1 collective-permute-done
  406.9 3.9 collective-permute-done.1
  410.8 0.7 copy.24
  411.5 0.7 copy.25
  (16 shorter events, 0.2 us)
Async XLA Ops:
  15.4 31.5 %all-to-all-start = ((f32[16,1,512]{2,1,0:T(1,128)}), f32[16,1,512]{2,1,0:T(1,128)S(1)}, u32[]{:S(2)}, u32[]{:S(2)}) async-start(f32[16,1,512]{2,1,0:T(1,128)} %broadcast_in_dim.10), calls=%async_computation | async-start | bytes 65536 | tf_op jit(solution)/shard_map/all_to_all | solution.py:16
  23.8 203.6 %reduce-scatter.3.cloned.1.call-start = ((), (), s32[]{:S(2)}) async-start(), calls=%async_computation.4 | async-start | bytes 26738688 | tf_op jit(solution)/shard_map/reduce_scatter | solution.py:98
  35.1 11.7 %copy-start.3 = (f32[1,768]{1,0:T(1,128)S(1)}, f32[1,768]{1,0:T(1,128)}, u32[]{:S(2)}) copy-start(f32[1,768]{1,0:T(1,128)} %param.16) | copy-start | bytes 9220
  35.1 11.8 %copy-start = (bf16[1,4,128,768]{3,2,1,0:T(8,128)(2,1)S(1)}, bf16[1,4,128,768]{3,2,1,0:T(8,128)(2,1)}, u32[]{:S(2)}) copy-start(bf16[1,4,128,768]{3,2,1,0:T(8,128)(2,1)} %param.9) | copy-start | bytes 2359300
  47.1 18.2 %slice-start = ((s8[12582912]{0:T(1024)(128)(4,1)}), s8[4194304]{0:T(1024)(128)(4,1)S(1)}, s32[]{:S(2)}) async-start(s8[12582912]{0:T(1024)(128)(4,1)} %bitcast.81), calls=%async_computation.7 | async-start | bytes 8388608
  57.5 7.8 %slice-start.1 = ((s8[12582912]{0:T(1024)(128)(4,1)}), s8[4194304]{0:T(1024)(128)(4,1)S(1)}, s32[]{:S(2)}) async-start(s8[12582912]{0:T(1024)(128)(4,1)} %bitcast.81), calls=%async_computation.8 | async-start | bytes 8388608
  57.5 7.8 %slice-start.2 = ((s8[12582912]{0:T(1024)(128)(4,1)}), s8[4194304]{0:T(1024)(128)(4,1)S(1)}, s32[]{:S(2)}) async-start(s8[12582912]{0:T(1024)(128)(4,1)} %bitcast.81), calls=%async_computation.9 | async-start | bytes 8388608
  73.9 153.4 %copy-start.2 = (f32[1,6144]{1,0:T(1,128)S(1)}, f32[1,6144]{1,0:T(1,128)}, u32[]{:S(2)}) copy-start(f32[1,6144]{1,0:T(1,128)} %param.13) | copy-start | bytes 73732
  74.0 246.9 %all-gather.3.cloned.1.call-start = ((), (), s32[]{:S(2)}) async-start(), calls=%async_computation.5 | async-start | bytes 13369344 | tf_op jit(solution)/shard_map/all_gather | solution.py:117
  231.4 154.6 %reduce-scatter.5.cloned.1.call-start = ((), (), s32[]{:S(2)}) async-start(), calls=%async_computation.6 | async-start | bytes 3932160 | tf_op jit(solution)/shard_map/reduce_scatter | solution.py:125
  320.9 10.8 %copy-start.5 = (bf16[512,2,6144]{2,0,1:T(8,128)(2,1)S(1)}, bf16[512,2,6144]{2,0,1:T(8,128)(2,1)}, u32[]{:S(2)}) copy-start(bf16[512,2,6144]{2,0,1:T(8,128)(2,1)} %all-gather.3.cloned.1.call-done) | copy-start | bytes 37748740
  339.3 55.1 %copy-start.4 = (f32[1,768]{1,0:T(1,128)S(1)}, f32[1,768]{1,0:T(1,128)}, u32[]{:S(2)}) copy-start(f32[1,768]{1,0:T(1,128)} %param.15) | copy-start | bytes 9220
  339.3 61.6 %copy-start.1 = (bf16[1,128,768]{2,1,0:T(8,128)(2,1)S(1)}, bf16[1,128,768]{2,1,0:T(8,128)(2,1)}, u32[]{:S(2)}) copy-start(bf16[1,128,768]{2,1,0:T(8,128)(2,1)} %param.11) | copy-start | bytes 589828
  387.8 13.1 %all-to-all-start.1 = ((f32[16,1,256]{2,1,0:T(1,128)}), f32[16,1,256]{2,1,0:T(1,128)S(1)}, u32[]{:S(2)}, u32[]{:S(2)}) async-start(f32[16,1,256]{2,1,0:T(1,128)} %broadcast_in_dim.24), calls=%async_computation.3 | async-start | bytes 32768 | tf_op jit(solution)/shard_map/all_to_all | solution.py:16
  402.3 4.6 %collective-permute-start = (bf16[128,768]{1,0:T(8,128)(2,1)S(1)}, bf16[128,768]{1,0:T(8,128)(2,1)S(1)}, u32[]{:S(2)}, u32[]{:S(2)}) collective-permute-start(bf16[128,768]{1,0:T(8,128)(2,1)S(1)} %get-tuple-element.13), channel_id=1, source_target_pairs={{0,64},{64,0},{1,65},{65,1},{2,66},{66,2},{3,67},{67,3},{4,68},{68... | collective-permute-start | bytes 589832 | tf_op jit(solution)/shard_map/ppermute | solution.py:33
  402.7 8.1 %collective-permute-start.1 = (bf16[128,768]{1,0:T(8,128)(2,1)S(1)}, bf16[128,768]{1,0:T(8,128)(2,1)S(1)}, u32[]{:S(2)}, u32[]{:S(2)}) collective-permute-start(bf16[128,768]{1,0:T(8,128)(2,1)S(1)} %get-tuple-element.12), channel_id=1, source_target_pairs={{0,64},{64,0},{1,65},{65,1},{2,66},{66,2},{3,67},{67,3},{4,68},{68... | collective-permute-start | bytes 589832 | tf_op jit(solution)/shard_map/ppermute | solution.py:33
Sparse Core Ops, SparseCore 0:
  74.1 153.2 reduce-scatter.2
  231.5 89.3 all-gather.2
  341.5 44.3 reduce-scatter.4
where the time goes:
time: 421 us; the launch traced here: 419 us
  waiting for transfers between devices  301 us (71%)
  matrix products  37.9 us (9%)
  blocking collectives  21.7 us (5%)
  other arithmetic  19.9 us (5%)
  between operations  17.8 us (4%)
  starting transfers between devices  16.7 us (4%)
    reduce_scatter x1, waiting for transfers between devices, body(): lax.psum_scatter(jnp.concatenate([jnp.dot(normed_all, w_first, preferred_...  153 us
    all_gather x1, waiting for transfers between devices, body(): piece = lax.all_gather(paired, 'col', axis=0, tiled=True)  89.5 us
    reduce_scatter x1, waiting for transfers between devices, body(): joint_out = lax.psum_scatter(terms, 'row', scatter_dimension=0, tiled=True)  44.5 us
    dot_general x2, matrix products, transposed(): lax.dot_general(left, right, (((1,), (1,)), ((), ())), preferred_element_...  19.3 us
    all_to_all x2, starting transfers between devices, copy_for_each(): return lax.all_to_all(copies, axis, split_axis=0, concat_axis=0, tiled=True)  15.1 us
    all_gather x1, blocking collectives, body(): lax.all_gather(upstream, 'row', axis=0, tiled=True)  11.3 us
    dot_general x1, matrix products, body(): jnp.dot(piece[:, 0], w_second, preferred_element_type=jnp.float32)  10.8 us
    all_gather x1, blocking collectives, body(): lax.all_gather(normed, 'row', axis=0, tiled=True)  10.3 us
  transfers between devices with their start and end apart: 7, of which 6 were waited for; matrix products, arithmetic and copies ran while one was open for 3% of the time, Pallas kernels for 0%

commit v1 on v0

v1 whole, which is shorter than its diff:
```python
import functools

import jax
import jax.numpy as jnp
from jax import lax
from jax.experimental import pallas as pl
from jax.experimental.pallas import tpu as pltpu
from jax.sharding import PartitionSpec as P

D = 12288
FT = 256
SIDE = 4
SLOTS = 8
SENDS = 4
BLK = 32

epsilon = 1e-05
root_coef = 0.7978845608028654
cubic_coef = 0.044715

RB1, D1, L1, RB2, D2, L2, A1, AR1, A2, AR2 = range(10)
KINDS = 10


def gelu_value(values):
    inner = root_coef * (values + cubic_coef * values * values * values)
    return 0.5 * values * (1.0 + jnp.tanh(inner))


def gelu_slope(values):
    inner = root_coef * (values + cubic_coef * values * values * values)
    tangent = jnp.tanh(inner)
    return 0.5 * (1.0 + tangent) + 0.5 * values * (1.0 - tangent * tangent) * root_coef * (
        1.0 + 3.0 * cubic_coef * values * values
    )


def dot_nn(a, b):
    return jnp.dot(a, b, preferred_element_type=jnp.float32)


def dot_nt(a, b):
    return lax.dot_general(a, b, (((1,), (1,)), ((), ())), preferred_element_type=jnp.float32)


def mid_kernel(
    lhs,
    stash,
    b_in,
    w_in,
    w_out,
    saved,
    out_fwd,
    out_bwd,
    win_s,
    wout_s,
    parts,
    rb1,
    lr1,
    quart,
    rb2,
    lr2,
    gath,
    acc,
    send_sem,
    recv_sem,
    win_sem,
    wout_sem,
):
    n_pair = win_s.shape[0] // 2
    ft = win_s.shape[2]
    units = 2 * n_pair
    f32, bf16 = jnp.float32, jnp.bfloat16
    col = lax.axis_index("col")
    pos = (col // SIDE, lax.rem(col, SIDE))

    def at_x(by):
        return {"col": lax.rem(pos[0] + by + SIDE, SIDE) * SIDE + pos[1]}

    def at_z(by):
        return {"col": pos[0] * SIDE + lax.rem(pos[1] + by + SIDE, SIDE)}

    hops = (at_x, at_z)

    def win_copy(t):
        return pltpu.make_async_copy(
            w_in.at[:, pl.ds(pl.multiple_of(t * ft, ft), ft)], win_s.at[t], win_sem.at[t]
        )

    def wout_copy(t):
        return pltpu.make_async_copy(
            w_out.at[pl.ds(pl.multiple_of(t * ft, ft), ft), :], wout_s.at[t], wout_sem.at[t]
        )

    @pl.loop(0, 2 * n_pair)
    def _(t):
        wout_copy(t).start()

    @pl.loop(0, 2 * n_pair)
    def _(t):
        win_copy(t).start()

    barrier = pltpu.get_barrier_semaphore()
    for hop in hops:
        for by in (1, -1):
            pl.semaphore_signal(
                barrier, inc=1, device_id=hop(by), device_id_type=pl.DeviceIdType.MESH
            )
    pl.semaphore_wait(barrier, 4)

    def ring(q, phase):
        axis = (q + phase) % 2
        return pos[axis], hops[axis]

    def wrap(v):
        return lax.rem(v + SIDE, SIDE)

    def copy(kind, q, u, d, src, dst, hop):
        return pltpu.make_async_remote_copy(
            src_ref=src,
            dst_ref=dst,
            send_sem=send_sem.at[kind, q, lax.rem(u, SENDS), d],
            recv_sem=recv_sem.at[kind, q, lax.rem(u, SLOTS), d],
            device_id=hop(1 if d == 0 else -1),
            device_id_type=pl.DeviceIdType.MESH,
        )

    def span(i, size, lo, n):
        return pl.ds(pl.multiple_of(i * size + lo, n), n)

    def scatter_copies(buf, back, side, size, kinds, me, hop, q, u):
        half = size // 2
        s = lax.rem(u, SLOTS)
        far, nxt, prv = wrap(me + 2), wrap(me + 1), wrap(me - 1)
        src = buf.at[q, s]
        relay = [
            copy(kinds[0], q, u, 0, src.at[span(far, size, 0, half)], back.at[q, s, 0], hop),
            copy(kinds[0], q, u, 1, src.at[span(far, size, half, half)], back.at[q, s, 1], hop),
        ]
        direct = [
            copy(kinds[1], q, u, 0, src.at[span(nxt, size, half, half)],
                 side.at[q, s, 0, pl.ds(half, half)], hop),
            copy(kinds[1], q, u, 1, src.at[span(prv, size, 0, half)],
                 side.at[q, s, 1, pl.ds(0, half)], hop),
        ]
        late = [
            copy(kinds[2], q, u, 0, src.at[span(nxt, size, 0, half)],
                 side.at[q, s, 0, pl.ds(0, half)], hop),
            copy(kinds[2], q, u, 1, src.at[span(prv, size, half, half)],
                 side.at[q, s, 1, pl.ds(half, half)], hop),
        ]
        return relay, direct, late

    def relay_step(buf, back, size, copies, me, q, u):
        relay, direct, late = copies
        half = size // 2
        s = lax.rem(u, SLOTS)
        for d, (chunk, lo) in enumerate(((wrap(me + 1), 0), (wrap(me - 1), half))):
            relay[d].wait_recv()
            rows = span(chunk, size, lo, half)
            buf[q, s, rows] = (
                buf[q, s, rows].astype(f32) + back[q, s, d].astype(f32)
            ).astype(bf16)
            late[d].start()
        for c in relay + direct:
            c.wait_send()

    big, small = SIDE * BLK, BLK

    def rs1(q, u):
        me, hop = ring(q, 0)
        return scatter_copies(parts, rb1, lr1, big, (RB1, D1, L1), me, hop, q, u)

    def rs2(q, u):
        me, hop = ring(q, 1)
        return scatter_copies(quart, rb2, lr2, small, (RB2, D2, L2), me, hop, q, u)

    def s0(u, q):
        s = lax.rem(u, SLOTS)

        @pl.when(u < n_pair)
        def _():
            t = 2 * u + q
            wout_copy(t).wait()
            parts[q, s] = dot_nt(lhs[0, q], wout_s[t]).astype(bf16)

        @pl.when(u >= n_pair)
        def _():
            t = 2 * (u - n_pair) + q
            parts[q, s] = dot_nn(lhs[1, q], win_s[t]).astype(bf16)

        relay, direct, _ = rs1(q, u)
        for c in relay + direct:
            c.start()

    def s1(u, q):
        me, _ = ring(q, 0)
        relay_step(parts, rb1, big, rs1(q, u), me, q, u)

    def s2(u, q):
        me, _ = ring(q, 0)
        s = lax.rem(u, SLOTS)
        _, direct, late = rs1(q, u)
        for c in direct + late:
            c.wait_recv()
        quart[q, s] = (
            parts[q, s, span(me, big, 0, big)].astype(f32)
            + lr1[q, s, 0].astype(f32)
            + lr1[q, s, 1].astype(f32)
        ).astype(bf16)
        relay, direct, _ = rs2(q, u)
        for c in relay + direct:
            c.start()
        for c in late:
            c.wait_send()

    def s3(u, q):
        me, _ = ring(q, 1)
        relay_step(quart, rb2, small, rs2(q, u), me, q, u)

    def gather1(q, u):
        me1, _ = ring(q, 0)
        me, hop = ring(q, 1)
        g = gath.at[q, lax.rem(u, SLOTS), me1]
        half = BLK // 2
        own = [copy(A1, q, u, d, g.at[me], g.at[me], hop) for d in (0, 1)]
        on = []
        for d, (b, lo) in enumerate(((wrap(me - 1), 0), (wrap(me + 1), half))):
            r = g.at[b, pl.ds(lo, half)]
            on.append(copy(AR1, q, u, d, r, r, hop))
        return own, on

    def gather2(q, u):
        me, hop = ring(q, 0)
        g = gath.at[q, lax.rem(u, SLOTS)]
        own = [copy(A2, q, u, d, g.at[me], g.at[me], hop) for d in (0, 1)]
        on = []
        for d, (b, lo) in enumerate(((wrap(me - 1), 0), (wrap(me + 1), SIDE // 2))):
            r = g.at[b, pl.ds(lo, SIDE // 2)]
            on.append(copy(AR2, q, u, d, r, r, hop))
        return own, on

    def s4(u, q):
        me1, _ = ring(q, 0)
        me2, _ = ring(q, 1)
        s = lax.rem(u, SLOTS)
        _, direct, late = rs2(q, u)
        for c in direct + late:
            c.wait_recv()
        h = (
            quart[q, s, span(me2, small, 0, small)].astype(f32)
            + lr2[q, s, 0].astype(f32)
            + lr2[q, s, 1].astype(f32)
        )

        @pl.when(u < n_pair)
        def _():
            t = 2 * u + q
            cols = pl.ds(pl.multiple_of(t * ft, ft), ft)
            slope = gelu_slope(stash[:, cols].astype(f32))
            gath[q, s, me1, me2] = (h * slope).astype(bf16)

        @pl.when(u >= n_pair)
        def _():
            t = 2 * (u - n_pair) + q
            cols = pl.ds(pl.multiple_of(t * ft, ft), ft)
            hidden = h + b_in[:, cols]
            saved[:, cols] = hidden.astype(bf16)
            gath[q, s, me1, me2] = gelu_value(hidden).astype(bf16)

        own, _ = gather1(q, u)
        for c in own:
            c.start()
        for c in late:
            c.wait_send()

    def pass_on(own, on):
        for d in (0, 1):
            own[d].wait_recv()
            on[d].start()
        for c in own:
            c.wait_send()

    def s5(u, q):
        pass_on(*gather1(q, u))

    def s6(u, q):
        _, on = gather1(q, u)
        for c in on:
            c.wait_recv()
        own, _ = gather2(q, u)
        for c in own:
            c.start()
        for c in on:
            c.wait_send()

    def s7(u, q):
        pass_on(*gather2(q, u))

    def s8(u, q):
        s = lax.rem(u, SLOTS)
        _, on = gather2(q, u)
        for c in on:
            c.wait_recv()
        for c in on:
            c.wait_send()
        rows = SIDE * SIDE * BLK
        piece = gath[q, s].reshape(rows, ft)

        def add(kind, first, value):
            @pl.when(first)
            def _():
                acc[kind, q] = value

            @pl.when(jnp.logical_not(first))
            def _():
                acc[kind, q] += value

        @pl.when(u < n_pair)
        def _():
            t = 2 * u + q
            win_copy(t).wait()
            add(0, u == 0, dot_nt(piece, win_s[t]))

        @pl.when(u >= n_pair)
        def _():
            t = 2 * (u - n_pair) + q
            add(1, u == n_pair, dot_nn(piece, wout_s[t]))

    stages = (s0, s1, s2, s3, s4, s5, s6, s7, s8)

    @pl.loop(0, units + len(stages) - 1)
    def _(step):
        for k, stage in enumerate(stages):
            u = step - k

            @pl.when(jnp.logical_and(u >= 0, u < units))
            def _():
                for q in (0, 1):
                    stage(u, q)

    @pl.loop(0, SIDE * SIDE)
    def _(b):
        x, z = b // SIDE, lax.rem(b, SIDE)
        rows = pl.ds(pl.multiple_of(b * BLK, BLK), BLK)
        swap = pl.ds(pl.multiple_of((z * SIDE + x) * BLK, BLK), BLK)
        out_bwd[rows] = (acc[0, 0, rows] + acc[0, 1, swap]).astype(out_bwd.dtype)
        out_fwd[rows] = (acc[1, 0, rows] + acc[1, 1, swap]).astype(out_fwd.dtype)


def mid(lhs, stash, b_in, w_in, w_out, ft=FT, out_dtype=jnp.bfloat16):
    feat, hid = w_in.shape
    tiles = hid // ft
    rows = SIDE * SIDE * BLK
    bf16 = jnp.bfloat16
    vmem, anyw = pl.BlockSpec(memory_space=pltpu.VMEM), pl.BlockSpec(memory_space=pl.ANY)
    flops = 8 * rows * feat * hid
    return pl.pallas_call(
        mid_kernel,
        out_shape=(
            jax.ShapeDtypeStruct((BLK, hid), bf16),
            jax.ShapeDtypeStruct((rows, feat), out_dtype),
            jax.ShapeDtypeStruct((rows, feat), out_dtype),
        ),
        in_specs=[vmem, vmem, vmem, anyw, anyw],
        out_specs=(vmem, vmem, vmem),
        scratch_shapes=[
            pltpu.VMEM((tiles, feat, ft), bf16),
            pltpu.VMEM((tiles, ft, feat), bf16),
            pltpu.VMEM((2, SLOTS, rows, ft), bf16),
            pltpu.VMEM((2, SLOTS, 2, 2 * BLK, ft), bf16),
            pltpu.VMEM((2, SLOTS, 2, 4 * BLK, ft), bf16),
            pltpu.VMEM((2, SLOTS, 4 * BLK, ft), bf16),
            pltpu.VMEM((2, SLOTS, 2, BLK // 2, ft), bf16),
            pltpu.VMEM((2, SLOTS, 2, BLK, ft), bf16),
            pltpu.VMEM((2, SLOTS, SIDE, SIDE, BLK, ft), bf16),
            pltpu.VMEM((2, 2, rows, feat), jnp.float32),
            pltpu.SemaphoreType.DMA((KINDS, 2, SENDS, 2)),
            pltpu.SemaphoreType.DMA((KINDS, 2, SLOTS, 2)),
            pltpu.SemaphoreType.DMA((tiles,)),
            pltpu.SemaphoreType.DMA((tiles,)),
        ],
        compiler_params=pltpu.CompilerParams(
            collective_id=0, has_side_effects=True, vmem_limit_bytes=67043328
        ),
        cost_estimate=pl.CostEstimate(
            flops=flops, bytes_accessed=4 * feat * hid, transcendentals=0
        ),
        name="mid",
    )(lhs, stash, b_in, w_in, w_out)


def copy_for_each(array, axis):
    copies = jnp.broadcast_to(array, (lax.axis_size(axis), *array.shape))
    return lax.all_to_all(copies, axis, split_axis=0, concat_axis=0, tiled=True)


def of_everyone(array, axis):
    return copy_for_each(array, axis).sum(axis=0)


def in_one(arrays, axis):
    ends = [0]
    for a in arrays:
        ends.append(ends[-1] + a.size)
    total = of_everyone(jnp.concatenate([a.ravel() for a in arrays]), axis)
    return tuple((total[b:e].reshape(a.shape) for a, b, e in zip(arrays, ends, ends[1:])))


def shifted(array, axis, by):
    size = lax.axis_size(axis)
    return lax.ppermute(array, axis, [(i, (i + by) % size) for i in range(size)])


def finish_norm(values, total, squares):
    mean_val = total / D
    sq_mean = squares / D
    inv_std = lax.rsqrt(sq_mean - mean_val * mean_val + epsilon)
    return ((values - mean_val[:, None]) * inv_std[:, None], inv_std)


def swapped(rows):
    return rows.reshape(SIDE, SIDE, BLK, -1).swapaxes(0, 1).reshape(rows.shape)


def body(stash_inputs, stash_hidden, grad_in, w_in, b_in, w_out, b_out, ln_gain, plan):
    bwd_slot = plan[0, 0]
    fwd_slot = plan[0, 1]
    fwd_input = lax.dynamic_index_in_dim(stash_inputs[0], fwd_slot, 0, keepdims=False).astype(
        jnp.float32
    )
    bwd_input = lax.dynamic_index_in_dim(stash_inputs[0], bwd_slot, 0, keepdims=False).astype(
        jnp.float32
    )
    bwd_hidden = lax.dynamic_index_in_dim(stash_hidden[0], bwd_slot, 0, keepdims=False)
    upstream = grad_in[0]
    gain_part = ln_gain[0]
    feat_part = w_out.shape[2]
    sums = in_one(
        (
            jnp.sum(fwd_input, axis=1),
            jnp.sum(fwd_input * fwd_input, axis=1),
            jnp.sum(bwd_input, axis=1),
            jnp.sum(bwd_input * bwd_input, axis=1),
        ),
        "col",
    )
    fwd_hat, fwd_inv = finish_norm(fwd_input, sums[0], sums[1])
    bwd_hat, bwd_inv = finish_norm(bwd_input, sums[2], sums[3])
    normed = (fwd_hat * gain_part).astype(jnp.bfloat16)
    normed_all = lax.all_gather(normed, "row", axis=0, tiled=True)
    upstream_all = lax.all_gather(upstream, "row", axis=0, tiled=True)
    lhs = jnp.stack([upstream_all, swapped(upstream_all), normed_all, swapped(normed_all)])
    lhs = lhs.reshape(2, 2, *normed_all.shape)
    saved, terms_f, terms_b = mid(lhs, bwd_hidden, b_in, w_in[0], w_out[0])
    joint_out = lax.psum_scatter(
        jnp.concatenate([terms_f, terms_b], axis=1), "row", scatter_dimension=0, tiled=True
    ).astype(jnp.float32)
    out_sum = joint_out[:, :feat_part]
    norm_grad = joint_out[:, feat_part:]
    output = (out_sum + b_out[0] + fwd_input).astype(jnp.bfloat16)
    scaled = norm_grad * gain_part
    grad_sums = in_one((jnp.sum(scaled, axis=1), jnp.sum(scaled * bwd_hat, axis=1)), "col")
    first_mean = grad_sums[0] / D
    second_mean = grad_sums[1] / D
    in_grad = upstream.astype(jnp.float32) + bwd_inv[:, None] * (
        scaled - first_mean[:, None] - bwd_hat * second_mean[:, None]
    )
    act_recv = shifted(output, "section", 1)
    grad_recv = shifted(in_grad.astype(jnp.bfloat16), "section", -1)
    return (act_recv[None], grad_recv[None], saved[None])


def solution(mesh):
    in_specs = (
        P("section", None, "row", "col"),
        P("section", None, "col", "row"),
        P("section", "row", "col"),
        P("section", "col", "row"),
        P("section", "row"),
        P("section", "row", "col"),
        P("section", "col"),
        P("section", "col"),
        P("section", None),
    )
    out_specs = (P("section", "row", "col"), P("section", "row", "col"), P("section", "col", "row"))
    return jax.shard_map(body, mesh=mesh, in_specs=in_specs, out_specs=out_specs, check_vma=False)
```

time: 421 us -> 273 us (0.65)
  waiting for transfers between devices: 301 us -> 51.9 us
  Pallas kernels: 0 us -> 146 us
  matrix products: 37.9 us -> 0 us
  other arithmetic: 19.9 us -> 10.2 us
    reduce_scatter x2 -> x1, waiting for transfers between devices: 198 us -> 38.6 us  [body(): lax.psum_scatter(jnp.concatenate([terms_f, terms_b], axis=1), 'row', scat...]
    pallas_call x0 -> x1, Pallas kernels: none -> 146 us  [mid(): pl.pallas_call(mid_kernel, out_shape=(jax.ShapeDtypeStruct((BLK, hid), bf...]
    all_gather x1 -> x0, waiting for transfers between devices: 89.5 us -> none  [body(): piece = lax.all_gather(paired, 'col', axis=0, tiled=True)]
    dot_general x4 -> x0, matrix products: 37.9 us -> none  [the longest x2 19.3 us: transposed(): lax.dot_general(left, right, (((1,), (1,)), ((), ())), preferred_element_...]
    concatenate x2 -> x1, other arithmetic: 10.7 us -> 2.71 us  [body(): jnp.concatenate([terms_f, terms_b], axis=1)]
  transfers between devices with their start and end apart: 7 -> 5, of which waited for: 6 -> 4; matrix products, arithmetic and copies ran while one was open for 3% -> 1% of each run, Pallas kernels for 0% -> 0%
where the time goes in v1:
time: 273 us; the launch traced here: 271 us
  Pallas kernels  146 us (53%)
  waiting for transfers between devices  51.9 us (19%)
  blocking collectives  21.5 us (8%)
  between operations  18.1 us (7%)
  starting transfers between devices  16.7 us (6%)
  other arithmetic  10.2 us (4%)
  local copies, waits for them, and re-layouts  6.6 us (2%)
    pallas_call x1, Pallas kernels, mid(): pl.pallas_call(mid_kernel, out_shape=(jax.ShapeDtypeStruct((BLK, hid), bf...  146 us
    reduce_scatter x1, waiting for transfers between devices, body(): lax.psum_scatter(jnp.concatenate([terms_f, terms_b], axis=1), 'row', scat...  38.6 us
    all_to_all x2, starting transfers between devices, copy_for_each(): return lax.all_to_all(copies, axis, split_axis=0, concat_axis=0, tiled=True)  15.1 us
    all_gather x1, blocking collectives, body(): upstream_all = lax.all_gather(upstream, 'row', axis=0, tiled=True)  11.3 us
    all_gather x1, blocking collectives, body(): normed_all = lax.all_gather(normed, 'row', axis=0, tiled=True)  10.2 us
    ppermute x2, waiting for transfers between devices, shifted(): lax.ppermute(array, axis, [(i, (i + by) % size) for i in range(size)])  6.94 us
    all_to_all x2, waiting for transfers between devices, copy_for_each(): return lax.all_to_all(copies, axis, split_axis=0, concat_axis=0, tiled=True)  6.42 us
  transfers between devices with their start and end apart: 5, of which 4 were waited for; matrix products, arithmetic and copies ran while one was open for 1% of the time, Pallas kernels for 0%

profile of v1, /device:TPU:1, one launch (start us, length us, event | category | flops | bytes accessed | tf_op | source)
XLA Modules:
  0.0 270.8 jit_solution(2806421693382934621)
XLA Ops:
  7.2 0.0 copy-start.7
  7.2 1.3 fusion.20
  12.4 1.2 convert_reduce_fusion.1
  13.5 1.2 fusion.5
  14.7 0.6 broadcast_in_dim.10
  15.4 8.4 %all-to-all-start = ((f32[16,1,512]{2,1,0:T(1,128)}), f32[16,1,512]{2,1,0:T(1,128)S(1)}, u32[]{:S(2)}, u32[]{:S(2)}) async-start(f32[16,1,512]{2,1,0:T(1,128)} %broadcast_in_dim.10), calls=%async_computation | async-start | bytes 65536 | tf_op jit(solution)/shard_map/all_to_all | solution.py:395
  23.8 0.0 reduce-scatter.2.cloned.1.call-start
  23.8 1.8 dynamic-slice_bitcast_fusion.stash
  25.6 11.3 %all-gather = bf16[1,512,768]{2,1,0:T(8,128)(2,1)S(1)} all-gather(bf16[1,128,768]{2,1,0:T(8,128)(2,1)} %param.11), channel_id=2, replica_groups=mesh['section'=2,'row'=4,'col'=16] {'row'}, dimensions={1}, use_global_device_ids=true | all-gather | bytes 983040 | tf_op jit(solution)/shard_map/all_gather | solution.py:452
  36.9 0.1 copy.16
  37.0 0.0 copy-done.7
  37.0 0.0 copy-start.3
  37.0 0.0 all-to-all-done
  37.1 0.6 slice_multiply_fusion.3
  37.6 1.1 fusion.8
  38.7 10.2 %all_gather.7 = bf16[512,768]{1,0:T(8,128)(2,1)S(1)} all-gather(bf16[128,768]{1,0:T(8,128)(2,1)S(1)} %fusion.8), channel_id=1, replica_groups=mesh['section'=2,'row'=4,'col'=16] {'row'}, dimensions={0}, use_global_device_ids=true | all-gather | bytes 983040 | tf_op jit(solution)/shard_map/all_gather | solution.py:451
  48.9 0.1 copy.18
  49.0 1.9 pad_maximum_fusion
  50.9 0.0 copy-done.3
  50.9 145.8 %mid.1 = (bf16[32,6144]{1,0:T(8,128)(2,1)}, bf16[512,768]{1,0:T(8,128)(2,1)}, bf16[512,768]{1,0:T(8,128)(2,1)}) custom-call(bf16[2,2,512,768]{3,2,1,0:T(8,128)(2,1)} %bitcast.69, bf16[32,6144]{1,0:T(8,128)(2,1)} %dynamic-slice_bitcast_fusion.stash, f32[1,6144]{1,0:T(1,128)} %b_in.1, bf16[768,6144]{1,0:T(8,128)(2,1)} %bitcast.73, bf16[6144,768]{1,0:T(8,128)(2,1)} %bitcast.74), custom_call_target="tpu_custom_call" | custom-call | flops 19327352832 | bytes 18874368 | tf_op jit(solution)/shard_map/mid/pallas_call | solution.py:358
  196.7 0.0 copy-start
  196.7 0.0 copy-start.4
  196.7 0.0 copy-start.5
  196.7 0.0 copy-start.6
  196.7 0.0 copy-start.8
  196.7 0.0 copy-start.1
  196.7 2.7 pad_maximum_fusion.1
  199.4 0.0 reduce-scatter.2.cloned.1.call-update
  199.5 38.6 %reduce-scatter.2.cloned.1.call-done = bf16[128,1536]{1,0:T(8,128)(2,1)} async-done(((bf16[512,1536]{1,0:T(8,128)(2,1)}), bf16[128,1536]{1,0:T(8,128)(2,1)}) %reduce-scatter.2.cloned.1.call-update) | async-done | bytes 393232 | tf_op jit(solution)/shard_map/reduce_scatter | solution.py:456
  238.0 1.1 convert_element_type.32
  239.1 0.0 copy-done
  239.1 0.0 copy-done.4
  239.1 0.0 copy-done.5
  239.1 0.0 copy-done.6
  239.1 0.2 fusion.19
  239.4 0.6 broadcast_in_dim.24
  240.0 6.7 %all-to-all-start.1 = ((f32[16,1,256]{2,1,0:T(1,128)}), f32[16,1,256]{2,1,0:T(1,128)S(1)}, u32[]{:S(2)}, u32[]{:S(2)}) async-start(f32[16,1,256]{2,1,0:T(1,128)} %broadcast_in_dim.24), calls=%async_computation.2 | async-start | bytes 32768 | tf_op jit(solution)/shard_map/all_to_all | solution.py:395
  246.7 0.0 copy-done.8
  246.7 6.4 %all-to-all-done.1 = f32[16,1,256]{2,1,0:T(1,128)S(1)} async-done(((f32[16,1,256]{2,1,0:T(1,128)}), f32[16,1,256]{2,1,0:T(1,128)S(1)}, u32[]{:S(2)}, u32[]{:S(2)}) %all-to-all-start.1) | async-done | bytes 16416 | tf_op jit(solution)/shard_map/all_to_all | solution.py:395
  253.2 0.0 copy-done.1
  253.2 0.2 fusion.18
  253.4 0.4 collective-permute-start
  253.8 1.2 collective-permute-start.1
  255.0 3.1 %collective-permute-done = bf16[128,768]{1,0:T(8,128)(2,1)S(1)} collective-permute-done((bf16[128,768]{1,0:T(8,128)(2,1)S(1)}, bf16[128,768]{1,0:T(8,128)(2,1)S(1)}, u32[]{:S(2)}, u32[]{:S(2)}) %collective-permute-start) | collective-permute-done | bytes 196640 | tf_op jit(solution)/shard_map/ppermute | solution.py:412
  258.0 3.9 %collective-permute-done.1 = bf16[128,768]{1,0:T(8,128)(2,1)S(1)} collective-permute-done((bf16[128,768]{1,0:T(8,128)(2,1)S(1)}, bf16[128,768]{1,0:T(8,128)(2,1)S(1)}, u32[]{:S(2)}, u32[]{:S(2)}) %collective-permute-start.1) | collective-permute-done | bytes 196640 | tf_op jit(solution)/shard_map/ppermute | solution.py:412
  261.9 0.7 copy.31
  262.6 0.7 copy.32
  263.3 0.7 copy.33
  (9 shorter events, 0.1 us)
Async XLA Ops:
  7.2 29.8 %copy-start.7 = (f32[1,768]{1,0:T(1,128)S(1)}, f32[1,768]{1,0:T(1,128)}, u32[]{:S(2)}) copy-start(f32[1,768]{1,0:T(1,128)} %param.16) | copy-start | bytes 9220
  15.4 21.6 %all-to-all-start = ((f32[16,1,512]{2,1,0:T(1,128)}), f32[16,1,512]{2,1,0:T(1,128)S(1)}, u32[]{:S(2)}, u32[]{:S(2)}) async-start(f32[16,1,512]{2,1,0:T(1,128)} %broadcast_in_dim.10), calls=%async_computation | async-start | bytes 65536 | tf_op jit(solution)/shard_map/all_to_all | solution.py:395
  23.8 214.2 %reduce-scatter.2.cloned.1.call-start = ((), (), s32[]{:S(2)}) async-start(), calls=%async_computation.3 | async-start | bytes 1966080 | tf_op jit(solution)/shard_map/reduce_scatter | solution.py:456
  37.0 13.9 %copy-start.3 = (f32[768]{0:T(1024)}, f32[768]{0:T(1024)S(1)}, u32[]{:S(2)}) copy-start(f32[768]{0:T(1024)S(1)} %reduce.4) | copy-start | bytes 9220
  196.7 42.4 %copy-start = (bf16[1,4,128,768]{3,2,1,0:T(8,128)(2,1)S(1)}, bf16[1,4,128,768]{3,2,1,0:T(8,128)(2,1)}, u32[]{:S(2)}) copy-start(bf16[1,4,128,768]{3,2,1,0:T(8,128)(2,1)} %param.9) | copy-start | bytes 2359300
  196.7 42.4 %copy-start.4 = (f32[768]{0:T(1024)S(1)}, f32[768]{0:T(1024)}, u32[]{:S(2)}) copy-start(f32[768]{0:T(1024)} %copy-done.3) | copy-start | bytes 9220
  196.7 42.4 %copy-start.5 = (f32[128]{0:T(128)S(1)}, f32[128]{0:T(128)}, u32[]{:S(2)}) copy-start(f32[128]{0:T(128)} %get-tuple-element.17) | copy-start | bytes 1540
  196.7 42.4 %copy-start.6 = (f32[128]{0:T(128)S(1)}, f32[128]{0:T(128)}, u32[]{:S(2)}) copy-start(f32[128]{0:T(128)} %get-tuple-element.18) | copy-start | bytes 1540
  196.7 50.0 %copy-start.8 = (f32[1,768]{1,0:T(1,128)S(1)}, f32[1,768]{1,0:T(1,128)}, u32[]{:S(2)}) copy-start(f32[1,768]{1,0:T(1,128)} %param.15) | copy-start | bytes 9220
  196.7 56.4 %copy-start.1 = (bf16[1,128,768]{2,1,0:T(8,128)(2,1)S(1)}, bf16[1,128,768]{2,1,0:T(8,128)(2,1)}, u32[]{:S(2)}) copy-start(bf16[1,128,768]{2,1,0:T(8,128)(2,1)} %param.11) | copy-start | bytes 589828
  199.4 63.8 %copy-start.2 = (bf16[32,6144]{1,0:T(8,128)(2,1)S(1)}, bf16[32,6144]{1,0:T(8,128)(2,1)}, u32[]{:S(2)}) copy-start(bf16[32,6144]{1,0:T(8,128)(2,1)} %get-tuple-element.8) | copy-start | bytes 1179652
  240.0 13.1 %all-to-all-start.1 = ((f32[16,1,256]{2,1,0:T(1,128)}), f32[16,1,256]{2,1,0:T(1,128)S(1)}, u32[]{:S(2)}, u32[]{:S(2)}) async-start(f32[16,1,256]{2,1,0:T(1,128)} %broadcast_in_dim.24), calls=%async_computation.2 | async-start | bytes 32768 | tf_op jit(solution)/shard_map/all_to_all | solution.py:395
  253.4 4.6 %collective-permute-start = (bf16[128,768]{1,0:T(8,128)(2,1)S(1)}, bf16[128,768]{1,0:T(8,128)(2,1)S(1)}, u32[]{:S(2)}, u32[]{:S(2)}) collective-permute-start(bf16[128,768]{1,0:T(8,128)(2,1)S(1)} %get-tuple-element.16), channel_id=1, source_target_pairs={{0,64},{64,0},{1,65},{65,1},{2,66},{66,2},{3,67},{67,3},{4,68},{68... | collective-permute-start | bytes 589832 | tf_op jit(solution)/shard_map/ppermute | solution.py:412
  253.8 8.1 %collective-permute-start.1 = (bf16[128,768]{1,0:T(8,128)(2,1)S(1)}, bf16[128,768]{1,0:T(8,128)(2,1)S(1)}, u32[]{:S(2)}, u32[]{:S(2)}) collective-permute-start(bf16[128,768]{1,0:T(8,128)(2,1)S(1)} %get-tuple-element.15), channel_id=1, source_target_pairs={{0,64},{64,0},{1,65},{65,1},{2,66},{66,2},{3,67},{67,3},{4,68},{68... | collective-permute-start | bytes 589832 | tf_op jit(solution)/shard_map/ppermute | solution.py:412
Sparse Core Ops, SparseCore 0:
  199.6 38.3 reduce-scatter.1

commit v2 on v1

--- a/solution.py
+++ b/solution.py
@@ -1,5 +1,3 @@
-import functools
-
 import jax
 import jax.numpy as jnp
 from jax import lax
@@ -43,15 +41,62 @@
     return lax.dot_general(a, b, (((1,), (1,)), ((), ())), preferred_element_type=jnp.float32)
 
 
-def mid_kernel(
-    lhs,
-    stash,
+class Copy:
+    def __init__(self, *args):
+        self.args = args
+
+    def make(self):
+        src, dst, send, recv, dev = self.args
+        return pltpu.make_async_remote_copy(
+            src_ref=src,
+            dst_ref=dst,
+            send_sem=send,
+            recv_sem=recv,
+            device_id=dev,
+            device_id_type=pl.DeviceIdType.MESH,
+        )
+
+    def start(self):
+        self.make().start()
+
+    def wait_recv(self):
+        self.make().wait_recv()
+
+    def wait_recv_into(self, dst):
+        src, _, send, recv, dev = self.args
+        Copy(dst, dst, send, recv, dev).wait_recv()
+
+    def wait_send(self):
+        self.make().wait_send()
+
+
+def step_kernel(
+    plan,
+    grad,
+    gain,
     b_in,
+    b_out,
+    stash_x,
+    stash_h,
     w_in,
     w_out,
+    act_recv,
+    grad_recv,
     saved,
-    out_fwd,
-    out_bwd,
+    lhs,
+    xs,
+    stash,
+    stat_src,
+    stat_in,
+    stats,
+    pair_src,
+    pair_in,
+    relay_in,
+    own_sum,
+    far_src,
+    far_in,
+    sect_src,
+    sect_in,
     win_s,
     wout_s,
     parts,
@@ -66,6 +111,9 @@
     recv_sem,
     win_sem,
     wout_sem,
+    load_sem,
+    side_send,
+    side_recv,
 ):
     n_pair = win_s.shape[0] // 2
     ft = win_s.shape[2]
@@ -84,29 +132,151 @@
 
     def win_copy(t):
         return pltpu.make_async_copy(
-            w_in.at[:, pl.ds(pl.multiple_of(t * ft, ft), ft)], win_s.at[t], win_sem.at[t]
+            w_in.at[0, :, pl.ds(pl.multiple_of(t * ft, ft), ft)], win_s.at[t], win_sem.at[t]
         )
 
     def wout_copy(t):
         return pltpu.make_async_copy(
-            w_out.at[pl.ds(pl.multiple_of(t * ft, ft), ft), :], wout_s.at[t], wout_sem.at[t]
+            w_out.at[0, pl.ds(pl.multiple_of(t * ft, ft), ft), :], wout_s.at[t], wout_sem.at[t]
         )
+
+    rows = SIDE * BLK
+    feat = win_s.shape[1]
+    row = lax.axis_index("row")
+    high, core = row // 2, lax.rem(row, 2)
+    section = lax.axis_index("section")
+    mate = {"row": high * 2 + 1 - core}
+    far = {"row": (1 - high) * 2 + core}
+    next_same = {"section": 1 - section, "row": row}
+    next_far = {"section": 1 - section, "row": (1 - high) * 2 + core}
+    everyone = [at_x(by) for by in (1, 2, 3)] + [at_z(by) for by in (1, 2, 3)]
+    everyone += [mate, far, next_same, next_far]
+
+    def side(i, src, dst, dev):
+        return Copy(src, dst, side_send.at[i], side_recv.at[i], dev)
+
+    loads = [
+        pltpu.make_async_copy(stash_x.at[0], xs, load_sem.at[0]),
+        pltpu.make_async_copy(stash_h.at[0], stash, load_sem.at[1]),
+    ]
+    loads[0].start()
 
     @pl.loop(0, 2 * n_pair)
     def _(t):
         wout_copy(t).start()
 
+    loads[1].start()
+
     @pl.loop(0, 2 * n_pair)
     def _(t):
         win_copy(t).start()
 
     barrier = pltpu.get_barrier_semaphore()
-    for hop in hops:
-        for by in (1, -1):
-            pl.semaphore_signal(
-                barrier, inc=1, device_id=hop(by), device_id_type=pl.DeviceIdType.MESH
-            )
-    pl.semaphore_wait(barrier, 4)
+    for dev in everyone:
+        pl.semaphore_signal(barrier, inc=1, device_id=dev, device_id_type=pl.DeviceIdType.MESH)
+    pl.semaphore_wait(barrier, len(everyone))
+
+    def row_block(high_of, core_of):
+        return pl.ds(pl.multiple_of((high_of * 2 + core_of) * rows, rows), rows)
+
+    half = rows // 2
+    mine, far_rows = row_block(high, core), row_block(1 - high, core)
+    grads = lhs.at[0, 0]
+
+    def half_of(block_high, n):
+        return pl.ds(pl.multiple_of((block_high * 2 + core) * rows + n * half, half), half)
+
+    to_mate = side(0, grad.at[0], grads.at[mine], mate)
+    out_hops = [
+        side(1 + n, grad.at[0, pl.ds(n * half, half)], relay_in.at[n], (next_same, next_far)[n])
+        for n in (0, 1)
+    ]
+    on_hops = [
+        side(3 + n, relay_in.at[n], grads.at[half_of(pass_high, n)], (next_far, next_same)[n])
+        for n, pass_high in ((0, high), (1, 1 - high))
+    ]
+    far_to_mate = [
+        side(5 + n, grads.at[half_of(1 - high, n)], grads.at[half_of(1 - high, n)], mate)
+        for n in (0, 1)
+    ]
+    for c in out_hops + [to_mate]:
+        c.start()
+    lhs[0, 0, mine] = grad[0]
+    for n in (0, 1):
+        out_hops[n].wait_recv()
+        on_hops[n].start()
+
+    def pack(columns):
+        lane = lax.broadcasted_iota(jnp.int32, (rows, rows), 1)
+        grid = jnp.zeros((rows, rows), f32)
+        for i, c in enumerate(columns):
+            grid = jnp.where(lane == i, c, grid)
+        return grid.T[:8]
+
+    def unpack(packed):
+        return jnp.concatenate([packed] * (rows // 8), axis=0).T
+
+    def stat_copies(n, axis):
+        hop = hops[axis]
+        first = 8 + (2 * n + axis) * 3
+        return [
+            side(first + j - 1, stat_src.at[n, axis], stat_in.at[n, axis, j - 1], hop(j))
+            for j in (1, 2, 3)
+        ]
+
+    def stat_send(n, axis, value):
+        stat_src[n, axis] = value
+        for c in stat_copies(n, axis):
+            c.start()
+
+    def stat_total(n, axis):
+        copies = stat_copies(n, axis)
+        for c in copies:
+            c.wait_recv()
+        total = stat_src[n, axis]
+        for j in (0, 1, 2):
+            total = total + stat_in[n, axis, j]
+        for c in copies:
+            c.wait_send()
+        return total
+
+    def row_sum(v):
+        return jnp.sum(v, axis=1, keepdims=True)
+
+    loads[0].wait()
+    fwd_input = xs[plan[0, 1]].astype(f32)
+    bwd_input = xs[plan[0, 0]].astype(f32)
+    stat_send(
+        0,
+        0,
+        pack(
+            [
+                row_sum(fwd_input),
+                row_sum(fwd_input * fwd_input),
+                row_sum(bwd_input),
+                row_sum(bwd_input * bwd_input),
+            ]
+        ),
+    )
+    loads[1].wait()
+
+    def swap_rows(k):
+        @pl.loop(0, SIDE * SIDE)
+        def _(b):
+            x, z = b // SIDE, lax.rem(b, SIDE)
+            lhs[k, 1, pl.ds(pl.multiple_of((z * SIDE + x) * BLK, BLK), BLK)] = lhs[
+                k, 0, pl.ds(pl.multiple_of(b * BLK, BLK), BLK)
+            ]
+
+    for n in (0, 1):
+        on_hops[n].wait_recv_into(grads.at[half_of(1 - high, n)])
+        far_to_mate[n].start()
+    to_mate.wait_recv()
+    for n in (0, 1):
+        far_to_mate[n].wait_recv()
+    swap_rows(0)
+    for c in out_hops + on_hops + far_to_mate + [to_mate]:
+        c.wait_send()
 
     def ring(q, phase):
         axis = (q + phase) % 2
@@ -116,13 +286,12 @@
         return lax.rem(v + SIDE, SIDE)
 
     def copy(kind, q, u, d, src, dst, hop):
-        return pltpu.make_async_remote_copy(
-            src_ref=src,
-            dst_ref=dst,
-            send_sem=send_sem.at[kind, q, lax.rem(u, SENDS), d],
-            recv_sem=recv_sem.at[kind, q, lax.rem(u, SLOTS), d],
-            device_id=hop(1 if d == 0 else -1),
-            device_id_type=pl.DeviceIdType.MESH,
+        return Copy(
+            src,
+            dst,
+            send_sem.at[kind, q, lax.rem(u, SENDS), d],
+            recv_sem.at[kind, q, lax.rem(u, SLOTS), d],
+            hop(1 if d == 0 else -1),
         )
 
     def span(i, size, lo, n):
@@ -257,7 +426,7 @@
         def _():
             t = 2 * u + q
             cols = pl.ds(pl.multiple_of(t * ft, ft), ft)
-            slope = gelu_slope(stash[:, cols].astype(f32))
+            slope = gelu_slope(stash[plan[0, 0], :, cols].astype(f32))
             gath[q, s, me1, me2] = (h * slope).astype(bf16)
 
         @pl.when(u >= n_pair)
@@ -265,7 +434,7 @@
             t = 2 * (u - n_pair) + q
             cols = pl.ds(pl.multiple_of(t * ft, ft), ft)
             hidden = h + b_in[:, cols]
-            saved[:, cols] = hidden.astype(bf16)
+            saved[0, :, cols] = hidden.astype(bf16)
             gath[q, s, me1, me2] = gelu_value(hidden).astype(bf16)
 
         own, _ = gather1(q, u)
@@ -328,6 +497,102 @@
             add(1, u == n_pair, dot_nn(piece, wout_s[t]))
 
     stages = (s0, s1, s2, s3, s4, s5, s6, s7, s8)
+    normed_rows = lhs.at[1, 0]
+    base = 20
+    normed_to_mate = side(base, normed_rows.at[mine], normed_rows.at[mine], mate)
+    normed_to_far = side(base + 1, normed_rows.at[mine], normed_rows.at[mine], far)
+    normed_on = side(base + 2, normed_rows.at[far_rows], normed_rows.at[far_rows], mate)
+    pair_sum = [side(base + 3 + k, pair_src.at[k], pair_in.at[k], mate) for k in (0, 1)]
+    far_sum = side(base + 5, far_src, far_in, far)
+    grad_on = side(base + 6, sect_src.at[0], sect_in.at[0], next_same)
+    act_on = [
+        side(base + 7, sect_src.at[1], sect_in.at[1], next_same),
+        side(base + 8, sect_src.at[2], sect_in.at[2], next_far),
+    ]
+
+    def total_rows(k, high_of, core_of):
+        r = high_of * 2 + core_of
+        pieces = []
+        for z in range(SIDE):
+            own = pl.ds(pl.multiple_of((r * SIDE + z) * BLK, BLK), BLK)
+            swap = pl.ds(pl.multiple_of((z * SIDE + r) * BLK, BLK), BLK)
+            pieces.append(acc[k, 0, own] + acc[k, 1, swap])
+        return jnp.concatenate(pieces, axis=0)
+
+    def send_pair(k):
+        for h in (0, 1):
+            pair_src[k, h] = total_rows(k, h, 1 - core).astype(bf16)
+        pair_sum[k].start()
+
+    def chip_rows(k, high_of):
+        return total_rows(k, high_of, core) + pair_in[k, high_of].astype(f32)
+
+    def norm_stats():
+        stat_send(0, 1, stat_total(0, 0))
+
+    def normalize():
+        total = unpack(stat_total(0, 1)) / D
+        mean_f, mean_b = total[:, 0:1], total[:, 2:3]
+        inv_f = lax.rsqrt(total[:, 1:2] - mean_f * mean_f + epsilon)
+        inv_b = lax.rsqrt(total[:, 3:4] - mean_b * mean_b + epsilon)
+        stats[0] = jnp.broadcast_to(mean_b, (rows, rows))
+        stats[1] = jnp.broadcast_to(inv_b, (rows, rows))
+        values = xs[plan[0, 1]].astype(f32)
+        lhs[1, 0, mine] = ((values - mean_f) * inv_f * gain[...]).astype(bf16)
+        normed_to_mate.start()
+        normed_to_far.start()
+
+    def normed_forward():
+        normed_to_far.wait_recv_into(normed_rows.at[far_rows])
+        normed_on.start()
+
+    def normed_done():
+        normed_to_mate.wait_recv()
+        normed_on.wait_recv()
+        swap_rows(1)
+        for c in (normed_to_mate, normed_to_far, normed_on):
+            c.wait_send()
+
+    def grad_far():
+        pair_sum[0].wait_recv()
+        own_sum[...] = chip_rows(0, high)
+        far_src[...] = chip_rows(0, 1 - high).astype(bf16)
+        far_sum.start()
+        pair_sum[0].wait_send()
+
+    def hat():
+        return (xs[plan[0, 0]].astype(f32) - stats[0, :, 0:1]) * stats[1, :, 0:1]
+
+    def grad_stats():
+        far_sum.wait_recv()
+        scaled = (own_sum[...] + far_in[...].astype(f32)) * gain[...]
+        own_sum[...] = scaled
+        stat_send(1, 0, pack([row_sum(scaled), row_sum(scaled * hat())]))
+        far_sum.wait_send()
+
+    def grad_stats_more():
+        stat_send(1, 1, stat_total(1, 0))
+
+    def grad_out():
+        total = unpack(stat_total(1, 1)) / D
+        in_grad = grad[0].astype(f32) + stats[1, :, 0:1] * (
+            own_sum[...] - total[:, 0:1] - hat() * total[:, 1:2]
+        )
+        sect_src[0] = in_grad.astype(bf16)
+        grad_on.start()
+
+    last = n_pair + len(stages) - 1
+    jobs = (
+        (2, norm_stats),
+        (4, normalize),
+        (7, normed_forward),
+        (9, normed_done),
+        (last, lambda: send_pair(0)),
+        (last + 1, grad_far),
+        (last + 4, grad_stats),
+        (last + 6, grad_stats_more),
+        (last + 8, grad_out),
+    )
 
     @pl.loop(0, units + len(stages) - 1)
     def _(step):
@@ -339,32 +604,57 @@
                 for q in (0, 1):
                     stage(u, q)
 
-    @pl.loop(0, SIDE * SIDE)
-    def _(b):
-        x, z = b // SIDE, lax.rem(b, SIDE)
-        rows = pl.ds(pl.multiple_of(b * BLK, BLK), BLK)
-        swap = pl.ds(pl.multiple_of((z * SIDE + x) * BLK, BLK), BLK)
-        out_bwd[rows] = (acc[0, 0, rows] + acc[0, 1, swap]).astype(out_bwd.dtype)
-        out_fwd[rows] = (acc[1, 0, rows] + acc[1, 1, swap]).astype(out_fwd.dtype)
-
-
-def mid(lhs, stash, b_in, w_in, w_out, ft=FT, out_dtype=jnp.bfloat16):
-    feat, hid = w_in.shape
+            if k == 0:
+                for at, job in jobs:
+                    pl.when(step == at)(job)
+
+    send_pair(1)
+    grad_on.wait_recv()
+    grad_recv[0] = sect_in[0]
+    residual = xs[plan[0, 1]].astype(f32) + b_out[...]
+    pair_sum[1].wait_recv()
+    sect_src[1] = (chip_rows(1, high) + residual).astype(bf16)
+    act_on[0].start()
+    sect_src[2] = chip_rows(1, 1 - high).astype(bf16)
+    act_on[1].start()
+    for c in act_on:
+        c.wait_recv()
+    act_recv[0] = (sect_in[1].astype(f32) + sect_in[2].astype(f32)).astype(bf16)
+    for c in act_on + [pair_sum[1], grad_on]:
+        c.wait_send()
+
+
+def body(stash_inputs, stash_hidden, grad_in, w_in, b_in, w_out, b_out, ln_gain, plan, ft=FT):
+    _, feat, hid = w_in.shape
+    slots = stash_inputs.shape[1]
     tiles = hid // ft
-    rows = SIDE * SIDE * BLK
-    bf16 = jnp.bfloat16
+    rows, mine = SIDE * SIDE * BLK, SIDE * BLK
+    bf16, f32 = jnp.bfloat16, jnp.float32
     vmem, anyw = pl.BlockSpec(memory_space=pltpu.VMEM), pl.BlockSpec(memory_space=pl.ANY)
-    flops = 8 * rows * feat * hid
     return pl.pallas_call(
-        mid_kernel,
+        step_kernel,
         out_shape=(
-            jax.ShapeDtypeStruct((BLK, hid), bf16),
-            jax.ShapeDtypeStruct((rows, feat), out_dtype),
-            jax.ShapeDtypeStruct((rows, feat), out_dtype),
+            jax.ShapeDtypeStruct((1, mine, feat), bf16),
+            jax.ShapeDtypeStruct((1, mine, feat), bf16),
+            jax.ShapeDtypeStruct((1, BLK, hid), bf16),
         ),
-        in_specs=[vmem, vmem, vmem, anyw, anyw],
+        in_specs=[pl.BlockSpec(memory_space=pltpu.SMEM), vmem, vmem, vmem, vmem] + [anyw] * 4,
         out_specs=(vmem, vmem, vmem),
         scratch_shapes=[
+            pltpu.VMEM((2, 2, rows, feat), bf16),
+            pltpu.VMEM((slots, mine, feat), bf16),
+            pltpu.VMEM((slots, BLK, hid), bf16),
+            pltpu.VMEM((2, 2, 8, mine), f32),
+            pltpu.VMEM((2, 2, 3, 8, mine), f32),
+            pltpu.VMEM((2, mine, mine), f32),
+            pltpu.VMEM((2, 2, mine, feat), bf16),
+            pltpu.VMEM((2, 2, mine, feat), bf16),
+            pltpu.VMEM((2, mine // 2, feat), bf16),
+            pltpu.VMEM((mine, feat), f32),
+            pltpu.VMEM((mine, feat), bf16),
+            pltpu.VMEM((mine, feat), bf16),
+            pltpu.VMEM((3, mine, feat), bf16),
+            pltpu.VMEM((3, mine, feat), bf16),
             pltpu.VMEM((tiles, feat, ft), bf16),
             pltpu.VMEM((tiles, ft, feat), bf16),
             pltpu.VMEM((2, SLOTS, rows, ft), bf16),
@@ -374,101 +664,20 @@
             pltpu.VMEM((2, SLOTS, 2, BLK // 2, ft), bf16),
             pltpu.VMEM((2, SLOTS, 2, BLK, ft), bf16),
             pltpu.VMEM((2, SLOTS, SIDE, SIDE, BLK, ft), bf16),
-            pltpu.VMEM((2, 2, rows, feat), jnp.float32),
+            pltpu.VMEM((2, 2, rows, feat), f32),
             pltpu.SemaphoreType.DMA((KINDS, 2, SENDS, 2)),
             pltpu.SemaphoreType.DMA((KINDS, 2, SLOTS, 2)),
             pltpu.SemaphoreType.DMA((tiles,)),
             pltpu.SemaphoreType.DMA((tiles,)),
+            pltpu.SemaphoreType.DMA((2,)),
+            pltpu.SemaphoreType.DMA((32,)),
+            pltpu.SemaphoreType.DMA((32,)),
         ],
         compiler_params=pltpu.CompilerParams(
             collective_id=0, has_side_effects=True, vmem_limit_bytes=67043328
         ),
-        cost_estimate=pl.CostEstimate(
-            flops=flops, bytes_accessed=4 * feat * hid, transcendentals=0
-        ),
-        name="mid",
-    )(lhs, stash, b_in, w_in, w_out)
-
-
-def copy_for_each(array, axis):
-    copies = jnp.broadcast_to(array, (lax.axis_size(axis), *array.shape))
-    return lax.all_to_all(copies, axis, split_axis=0, concat_axis=0, tiled=True)
-
-
-def of_everyone(array, axis):
-    return copy_for_each(array, axis).sum(axis=0)
-
-
-def in_one(arrays, axis):
-    ends = [0]
-    for a in arrays:
-        ends.append(ends[-1] + a.size)
-    total = of_everyone(jnp.concatenate([a.ravel() for a in arrays]), axis)
-    return tuple((total[b:e].reshape(a.shape) for a, b, e in zip(arrays, ends, ends[1:])))
-
-
-def shifted(array, axis, by):
-    size = lax.axis_size(axis)
-    return lax.ppermute(array, axis, [(i, (i + by) % size) for i in range(size)])
-
-
-def finish_norm(values, total, squares):
-    mean_val = total / D
-    sq_mean = squares / D
-    inv_std = lax.rsqrt(sq_mean - mean_val * mean_val + epsilon)
-    return ((values - mean_val[:, None]) * inv_std[:, None], inv_std)
-
-
-def swapped(rows):
-    return rows.reshape(SIDE, SIDE, BLK, -1).swapaxes(0, 1).reshape(rows.shape)
-
-
-def body(stash_inputs, stash_hidden, grad_in, w_in, b_in, w_out, b_out, ln_gain, plan):
-    bwd_slot = plan[0, 0]
-    fwd_slot = plan[0, 1]
-    fwd_input = lax.dynamic_index_in_dim(stash_inputs[0], fwd_slot, 0, keepdims=False).astype(
-        jnp.float32
-    )
-    bwd_input = lax.dynamic_index_in_dim(stash_inputs[0], bwd_slot, 0, keepdims=False).astype(
-        jnp.float32
-    )
-    bwd_hidden = lax.dynamic_index_in_dim(stash_hidden[0], bwd_slot, 0, keepdims=False)
-    upstream = grad_in[0]
-    gain_part = ln_gain[0]
-    feat_part = w_out.shape[2]
-    sums = in_one(
-        (
-            jnp.sum(fwd_input, axis=1),
-            jnp.sum(fwd_input * fwd_input, axis=1),
-            jnp.sum(bwd_input, axis=1),
-            jnp.sum(bwd_input * bwd_input, axis=1),
-        ),
-        "col",
-    )
-    fwd_hat, fwd_inv = finish_norm(fwd_input, sums[0], sums[1])
-    bwd_hat, bwd_inv = finish_norm(bwd_input, sums[2], sums[3])
-    normed = (fwd_hat * gain_part).astype(jnp.bfloat16)
-    normed_all = lax.all_gather(normed, "row", axis=0, tiled=True)
-    upstream_all = lax.all_gather(upstream, "row", axis=0, tiled=True)
-    lhs = jnp.stack([upstream_all, swapped(upstream_all), normed_all, swapped(normed_all)])
-    lhs = lhs.reshape(2, 2, *normed_all.shape)
-    saved, terms_f, terms_b = mid(lhs, bwd_hidden, b_in, w_in[0], w_out[0])
-    joint_out = lax.psum_scatter(
-        jnp.concatenate([terms_f, terms_b], axis=1), "row", scatter_dimension=0, tiled=True
-    ).astype(jnp.float32)
-    out_sum = joint_out[:, :feat_part]
-    norm_grad = joint_out[:, feat_part:]
-    output = (out_sum + b_out[0] + fwd_input).astype(jnp.bfloat16)
-    scaled = norm_grad * gain_part
-    grad_sums = in_one((jnp.sum(scaled, axis=1), jnp.sum(scaled * bwd_hat, axis=1)), "col")
-    first_mean = grad_sums[0] / D
-    second_mean = grad_sums[1] / D
-    in_grad = upstream.astype(jnp.float32) + bwd_inv[:, None] * (
-        scaled - first_mean[:, None] - bwd_hat * second_mean[:, None]
-    )
-    act_recv = shifted(output, "section", 1)
-    grad_recv = shifted(in_grad.astype(jnp.bfloat16), "section", -1)
-    return (act_recv[None], grad_recv[None], saved[None])
+        name="section_step",
+    )(plan, grad_in, ln_gain, b_in, b_out, stash_inputs, stash_hidden, w_in, w_out)
 
 
 def solution(mesh):

time: 273 us -> 177 us (0.65)
  waiting for transfers between devices: 51.9 us -> 0 us
  Pallas kernels: 146 us -> 171 us
  blocking collectives: 21.5 us -> 0 us
  between operations: 18.1 us -> 0.64 us
  starting transfers between devices: 16.7 us -> 0 us
  other arithmetic: 10.2 us -> 0 us
    reduce_scatter x1 -> x0, waiting for transfers between devices: 38.6 us -> none  [body(): lax.psum_scatter(jnp.concatenate([terms_f, terms_b], axis=1), 'row', scat...]
    pallas_call x1, Pallas kernels: 146 us -> 171 us  [body(): pl.pallas_call(step_kernel, out_shape=(jax.ShapeDtypeStruct((1, mine, fea...]
    all_gather x2 -> x0, blocking collectives: 21.5 us -> none  [the longest x1 11.3 us: body(): upstream_all = lax.all_gather(upstream, 'row', axis=0, tiled=True)]
    all_to_all x2 -> x0, starting transfers between devices: 15.1 us -> none  [copy_for_each(): return lax.all_to_all(copies, axis, split_axis=0, concat_axis=0, tiled=True)]
    ppermute x2 -> x0, waiting for transfers between devices: 6.94 us -> none  [shifted(): lax.ppermute(array, axis, [(i, (i + by) % size) for i in range(size)])]
    all_to_all x2 -> x0, waiting for transfers between devices: 6.42 us -> none  [copy_for_each(): return lax.all_to_all(copies, axis, split_axis=0, concat_axis=0, tiled=True)]
    unnamed x21 -> x3, local copies, waits for them, and re-layouts: 2.15 us -> 5 us
  transfers between devices with their start and end apart: 5 -> 0, of which waited for: 4 -> 0; matrix products, arithmetic and copies ran while one was open for 1% -> 0% of each run, Pallas kernels for 0% -> 0%
where the time goes in v2:
time: 177 us; the launch traced here: 176 us
  Pallas kernels  171 us (97%)
  local copies, waits for them, and re-layouts  5 us (3%)
    pallas_call x1, Pallas kernels, body(): pl.pallas_call(step_kernel, out_shape=(jax.ShapeDtypeStruct((1, mine, fea...  171 us
    unnamed x3, local copies, waits for them, and re-layouts  5 us

profile of v2, /device:TPU:1, one launch (start us, length us, event | category | flops | bytes accessed | tf_op | source)
XLA Modules:
  0.0 176.4 jit_solution(9875449918933087170)
XLA Ops:
  0.6 170.7 %section_step.1 = (bf16[1,128,768]{2,1,0:T(8,128)(2,1)}, bf16[1,128,768]{2,1,0:T(8,128)(2,1)}, bf16[1,32,6144]{2,1,0:T(8,128)(2,1)}) custom-call(s32[1,2]{1,0:T(1,128)} %plan.1, bf16[1,128,768]{2,1,0:T(8,128)(2,1)} %grad.1, f32[1,768]{1,0:T(1,128)} %gain.1, f32[1,6144]{1,0:T(1,128)} %b_in.1, f32[1,768]{1,0:T(1,128)} %b_out.1, ...), custom_call_target="tpu_custom_call" | custom-call | tf_op jit(solution)/shard_map/section_step/pallas_call | solution.py:634
  171.4 1.6 copy.15
  173.0 1.6 copy.16
  174.6 1.8 %copy.17 = bf16[1,32,6144]{2,1,0:T(8,128)(2,1)} copy(bf16[1,32,6144]{2,1,0:T(8,128)(2,1)} %get-tuple-element.8) | data formatting | bytes 786432

commit v3 on v2

v3 whole, which is shorter than its diff:
```python
import jax
import jax.numpy as jnp
from jax import lax
from jax.experimental import pallas as pl
from jax.experimental.pallas import tpu as pltpu
from jax.sharding import PartitionSpec as P

D = 12288
FT = 512
SIDE = 4
SLOTS = 8
LOCAL = 4
BLK = 32
LATE_STAGE = 8
PIECES = 8
PARTS = 3
FRONT = 32

epsilon = 1e-05
root_coef = 0.7978845608028654
cubic_coef = 0.044715

RB1, LR1, RB2, LR2, A1, AR1, A2, AR2 = range(8)
SEND_RING = (0, 0, 1, 1, 2, 2, 3, 3)


def gelu_value(values):
    inner = root_coef * (values + cubic_coef * values * values * values)
    return 0.5 * values * (1.0 + jnp.tanh(inner))


def gelu_slope(values):
    inner = root_coef * (values + cubic_coef * values * values * values)
    tangent = jnp.tanh(inner)
    return 0.5 * (1.0 + tangent) + 0.5 * values * (1.0 - tangent * tangent) * root_coef * (
        1.0 + 3.0 * cubic_coef * values * values
    )


def dot_nn(a, b):
    return jnp.dot(a, b, preferred_element_type=jnp.float32)


def dot_nt(a, b):
    return lax.dot_general(a, b, (((1,), (1,)), ((), ())), preferred_element_type=jnp.float32)


class Copy:
    def __init__(self, *args):
        self.args = args

    def make(self):
        src, dst, send, recv, dev = self.args
        return pltpu.make_async_remote_copy(
            src_ref=src,
            dst_ref=dst,
            send_sem=send,
            recv_sem=recv,
            device_id=dev,
            device_id_type=pl.DeviceIdType.MESH,
        )

    def start(self):
        self.make().start()

    def wait_recv(self):
        self.make().wait_recv()

    def wait_recv_into(self, dst):
        src, _, send, recv, dev = self.args
        Copy(dst, dst, send, recv, dev).wait_recv()

    def wait_send(self):
        self.make().wait_send()


def step_kernel(
    plan,
    grad,
    gain,
    b_in,
    b_out,
    stash_x,
    stash_h,
    w_in,
    w_out,
    act_recv,
    grad_recv,
    saved,
    lhs,
    xs,
    stash,
    stat_src,
    stat_in,
    stats,
    pair_src,
    pair_in,
    relay_in,
    own_sum,
    far_src,
    far_in,
    sect_src,
    sect_in,
    win_s,
    wout_s,
    parts,
    rb1,
    lr1,
    quart,
    rb2,
    lr2,
    gath,
    acc,
    send_sem,
    recv_sem,
    win_sem,
    wout_sem,
    load_sem,
    side_send,
    side_recv,
):
    n_pair = win_s.shape[0] // 2
    ft = win_s.shape[2]
    units = 2 * n_pair
    f32, bf16 = jnp.float32, jnp.bfloat16
    col = lax.axis_index("col")
    pos = (col // SIDE, lax.rem(col, SIDE))

    def wrap(v):
        return jnp.bitwise_and(v + SIDE, SIDE - 1)

    along = (
        [{"col": wrap(pos[0] + by) * SIDE + pos[1]} for by in (1, 2, 3)],
        [{"col": pos[0] * SIDE + wrap(pos[1] + by)} for by in (1, 2, 3)],
    )
    hops = tuple((ring[0], ring[2]) for ring in along)
    places = tuple((p, wrap(p + 1), wrap(p + 2), wrap(p + 3)) for p in pos)

    def slot(u):
        return jnp.bitwise_and(u, SLOTS - 1)

    def local(u):
        return jnp.bitwise_and(u, LOCAL - 1)

    def win_copy(t):
        return pltpu.make_async_copy(
            w_in.at[0, :, pl.ds(pl.multiple_of(t * ft, ft), ft)], win_s.at[t], win_sem.at[t]
        )

    def wout_copy(t):
        return pltpu.make_async_copy(
            w_out.at[0, pl.ds(pl.multiple_of(t * ft, ft), ft), :], wout_s.at[t], wout_sem.at[t]
        )

    rows = SIDE * BLK
    feat = win_s.shape[1]
    row = lax.axis_index("row")
    high, core = row // 2, lax.rem(row, 2)
    section = lax.axis_index("section")
    mate = {"row": high * 2 + 1 - core}
    far = {"row": (1 - high) * 2 + core}
    next_same = {"section": 1 - section, "row": row}
    next_far = {"section": 1 - section, "row": (1 - high) * 2 + core}
    everyone = [*along[0], *along[1], mate, far, next_same, next_far]

    def side(i, src, dst, dev):
        return Copy(src, dst, side_send.at[i], side_recv.at[i], dev)

    loads = [
        pltpu.make_async_copy(stash_x.at[0], xs, load_sem.at[0]),
        pltpu.make_async_copy(stash_h.at[0], stash, load_sem.at[1]),
    ]
    loads[0].start()

    @pl.loop(0, 2 * n_pair)
    def _(t):
        wout_copy(t).start()

    loads[1].start()

    @pl.loop(0, 2 * n_pair)
    def _(t):
        win_copy(t).start()

    barrier = pltpu.get_barrier_semaphore()
    for dev in everyone:
        pl.semaphore_signal(barrier, inc=1, device_id=dev, device_id_type=pl.DeviceIdType.MESH)
    pl.semaphore_wait(barrier, len(everyone))

    def row_block(high_of, core_of):
        return pl.ds(pl.multiple_of((high_of * 2 + core_of) * rows, rows), rows)

    piece = rows // PIECES
    mine, far_rows = row_block(high, core), row_block(1 - high, core)
    grads = lhs.at[0, 0]

    def piece_of(block_high, n):
        return pl.ds(pl.multiple_of((block_high * 2 + core) * rows + n * piece, piece), piece)

    by_way = (next_same, next_far)
    to_mate = side(0, grad.at[0], grads.at[mine], mate)
    out_hops = [
        side(FRONT + n, grad.at[0, pl.ds(n * piece, piece)], relay_in.at[n], by_way[n % 2])
        for n in range(PIECES)
    ]
    on_hops = [
        side(
            FRONT + PIECES + n,
            relay_in.at[n],
            grads.at[piece_of((high, 1 - high)[n % 2], n)],
            by_way[1 - n % 2],
        )
        for n in range(PIECES)
    ]
    far_to_mate = [
        side(
            FRONT + 2 * PIECES + n,
            grads.at[piece_of(1 - high, n)],
            grads.at[piece_of(1 - high, n)],
            mate,
        )
        for n in range(PIECES)
    ]
    for c in out_hops + [to_mate]:
        c.start()
    lhs[0, 0, mine] = grad[0]
    for n in range(PIECES):
        out_hops[n].wait_recv()
        on_hops[n].start()

    def pack(columns):
        lane = lax.broadcasted_iota(jnp.int32, (rows, rows), 1)
        grid = jnp.zeros((rows, rows), f32)
        for i, c in enumerate(columns):
            grid = jnp.where(lane == i, c, grid)
        return grid.T[:8]

    def unpack(packed):
        return jnp.concatenate([packed] * (rows // 8), axis=0).T

    def stat_copies(n, axis):
        first = 8 + (2 * n + axis) * 3
        return [
            side(first + j - 1, stat_src.at[n, axis], stat_in.at[n, axis, j - 1], along[axis][j - 1])
            for j in (1, 2, 3)
        ]

    def stat_send(n, axis, value):
        stat_src[n, axis] = value
        for c in stat_copies(n, axis):
            c.start()

    def stat_total(n, axis):
        copies = stat_copies(n, axis)
        for c in copies:
            c.wait_recv()
        total = stat_src[n, axis]
        for j in (0, 1, 2):
            total = total + stat_in[n, axis, j]
        for c in copies:
            c.wait_send()
        return total

    def row_sum(v):
        return jnp.sum(v, axis=1, keepdims=True)

    loads[0].wait()
    fwd_input = xs[plan[0, 1]].astype(f32)
    bwd_input = xs[plan[0, 0]].astype(f32)
    stat_send(
        0,
        0,
        pack(
            [
                row_sum(fwd_input),
                row_sum(fwd_input * fwd_input),
                row_sum(bwd_input),
                row_sum(bwd_input * bwd_input),
            ]
        ),
    )
    loads[1].wait()

    def swap_rows(k, r):
        for z in range(SIDE):
            lhs[k, 1, pl.ds(pl.multiple_of((z * SIDE + r) * BLK, BLK), BLK)] = lhs[
                k, 0, pl.ds(pl.multiple_of((r * SIDE + z) * BLK, BLK), BLK)
            ]

    far_row = (1 - high) * 2 + core
    mate_row, far_mate_row = high * 2 + 1 - core, (1 - high) * 2 + 1 - core
    swap_rows(0, row)
    for n in range(PIECES):
        on_hops[n].wait_recv_into(grads.at[piece_of(1 - high, n)])
        far_to_mate[n].start()
    to_mate.wait_recv()
    swap_rows(0, mate_row)
    swap_rows(0, far_row)
    for n in range(PIECES):
        far_to_mate[n].wait_recv()
    swap_rows(0, far_mate_row)
    for c in out_hops + on_hops + far_to_mate + [to_mate]:
        c.wait_send()

    def ring(q, phase):
        axis = (q + phase) % 2
        return places[axis], hops[axis]

    def copy(kind, q, u, d, src, dst, hop):
        return Copy(
            src,
            dst,
            send_sem.at[SEND_RING[kind], q, local(u)],
            recv_sem.at[kind, q, slot(u)],
            hop[d],
        )

    def arrived(kind, q, u, ref):
        Copy(ref, ref, send_sem.at[0, q, 0], recv_sem.at[kind, q, slot(u)], hops[0][0]).wait_recv()

    def all_sent(ring_no, q, u, ref):
        Copy(ref, ref, send_sem.at[ring_no, q, local(u)], recv_sem.at[0, q, 0], hops[0][0]).wait_send()

    def span(i, size, lo, n):
        return pl.ds(pl.multiple_of(i * size + lo, n), n)

    def scatter_first(buf, back, side_buf, size, kinds, place, hop, q, u):
        half = size // 2
        me, nxt, far_one, prv = place
        src, s = buf.at[q, local(u)], slot(u)
        copy(kinds[0], q, u, 0, src.at[span(far_one, size, 0, half)], back.at[q, s, 0], hop).start()
        copy(kinds[0], q, u, 1, src.at[span(far_one, size, half, half)], back.at[q, s, 1], hop).start()
        copy(kinds[1], q, u, 0, src.at[span(nxt, size, half, half)],
             side_buf.at[q, s, 0, pl.ds(half, half)], hop).start()
        copy(kinds[1], q, u, 1, src.at[span(prv, size, 0, half)],
             side_buf.at[q, s, 1, pl.ds(0, half)], hop).start()

    def scatter_relay(buf, back, side_buf, size, kinds, place, hop, q, u):
        half = size // 2
        me, nxt, far_one, prv = place
        l, s = local(u), slot(u)
        arrived(kinds[0], q, u, back.at[q, s])
        for d, (chunk, lo) in enumerate(((nxt, 0), (prv, half))):
            rows = span(chunk, size, lo, half)
            buf[q, l, rows] = (
                buf[q, l, rows].astype(f32) + back[q, s, d].astype(f32)
            ).astype(bf16)
            copy(kinds[1], q, u, d, buf.at[q, l, rows],
                 side_buf.at[q, s, d, pl.ds(lo, half)], hop).start()

    big, small = SIDE * BLK, BLK

    def s0(u, q):
        l = local(u)

        @pl.when(u < n_pair)
        def _():
            t = 2 * u + q
            wout_copy(t).wait()
            parts[q, l] = dot_nt(lhs[0, q], wout_s[t]).astype(bf16)

        @pl.when(u >= n_pair)
        def _():
            t = 2 * (u - n_pair) + q
            if n_pair < LATE_STAGE - 1:
                win_copy(t).wait()
            parts[q, l] = dot_nn(lhs[1, q], win_s[t]).astype(bf16)

        scatter_first(parts, rb1, lr1, big, (RB1, LR1), *ring(q, 0), q, u)

    def s1(u, q):
        scatter_relay(parts, rb1, lr1, big, (RB1, LR1), *ring(q, 0), q, u)

    def s2(u, q):
        place, _ = ring(q, 0)
        l, s = local(u), slot(u)
        arrived(LR1, q, u, lr1.at[q, s])
        quart[q, l] = (
            parts[q, l, span(place[0], big, 0, big)].astype(f32)
            + lr1[q, s, 0].astype(f32)
            + lr1[q, s, 1].astype(f32)
        ).astype(bf16)
        scatter_first(quart, rb2, lr2, small, (RB2, LR2), *ring(q, 1), q, u)
        all_sent(0, q, u, parts.at[q, l, pl.ds(0, 3 * big)])

    def s3(u, q):
        scatter_relay(quart, rb2, lr2, small, (RB2, LR2), *ring(q, 1), q, u)

    def s4(u, q):
        me1 = ring(q, 0)[0][0]
        place, hop = ring(q, 1)
        me2 = place[0]
        l, s = local(u), slot(u)
        arrived(LR2, q, u, lr2.at[q, s])
        h = (
            quart[q, l, span(me2, small, 0, small)].astype(f32)
            + lr2[q, s, 0].astype(f32)
            + lr2[q, s, 1].astype(f32)
        )

        @pl.when(u < n_pair)
        def _():
            t = 2 * u + q
            cols = pl.ds(pl.multiple_of(t * ft, ft), ft)
            slope = gelu_slope(stash[plan[0, 0], :, cols].astype(f32))
            gath[q, s, me1, me2] = (h * slope).astype(bf16)

        @pl.when(u >= n_pair)
        def _():
            t = 2 * (u - n_pair) + q
            cols = pl.ds(pl.multiple_of(t * ft, ft), ft)
            hidden = h + b_in[:, cols]
            saved[0, :, cols] = hidden.astype(bf16)
            gath[q, s, me1, me2] = gelu_value(hidden).astype(bf16)

        g = gath.at[q, s, me1, me2]
        for d in (0, 1):
            copy(A1, q, u, d, g, g, hop).start()
        all_sent(1, q, u, quart.at[q, l, pl.ds(0, 3 * small)])

    def s5(u, q):
        me1 = ring(q, 0)[0][0]
        place, hop = ring(q, 1)
        g = gath.at[q, slot(u), me1]
        arrived(A1, q, u, g.at[pl.ds(0, 2)])
        for d, (b, lo) in enumerate(((place[3], 0), (place[1], BLK // 2))):
            r = g.at[b, pl.ds(lo, BLK // 2)]
            copy(AR1, q, u, d, r, r, hop).start()

    def product(u, q, blocks):
        s = slot(u)

        def add(kind, first, values):
            @pl.when(first)
            def _():
                for b, value in zip(blocks, values):
                    acc[kind, q, span(b, big, 0, big)] = value

            @pl.when(jnp.logical_not(first))
            def _():
                for b, value in zip(blocks, values):
                    acc[kind, q, span(b, big, 0, big)] += value

        pieces = [gath[q, s, b].reshape(big, ft) for b in blocks]

        @pl.when(u < n_pair)
        def _():
            t = 2 * u + q
            add(0, u == 0, [dot_nt(piece, win_s[t]) for piece in pieces])

        @pl.when(u >= n_pair)
        def _():
            t = 2 * (u - n_pair) + q
            add(1, u == n_pair, [dot_nn(piece, wout_s[t]) for piece in pieces])

    def s6(u, q):
        place, hop = ring(q, 0)
        me1 = place[0]
        g = gath.at[q, slot(u)]
        arrived(AR1, q, u, g.at[me1, 0])
        for d in (0, 1):
            copy(A2, q, u, d, g.at[me1], g.at[me1], hop).start()
        if n_pair >= LATE_STAGE - 1:

            @pl.when(u < n_pair)
            def _():
                win_copy(2 * u + q).wait()

        product(u, q, [me1])
        all_sent(2, q, u, g.at[me1, pl.ds(0, 3)])

    def s7(u, q):
        place, hop = ring(q, 0)
        g = gath.at[q, slot(u)]
        arrived(A2, q, u, g.at[pl.ds(0, 2)])
        for d, (b, lo) in enumerate(((place[3], 0), (place[1], SIDE // 2))):
            r = g.at[b, pl.ds(lo, SIDE // 2)]
            copy(AR2, q, u, d, r, r, hop).start()
        product(u, q, [place[1], place[3]])

    def s8(u, q):
        place, _ = ring(q, 0)
        g = gath.at[q, slot(u)]
        arrived(AR2, q, u, g.at[0])
        product(u, q, [place[2]])
        all_sent(3, q, u, g.at[pl.ds(0, 3)])

    stages = (s0, s1, s2, s3, s4, s5, s6, s7, s8)
    normed_rows = lhs.at[1, 0]
    base = 20
    normed_to_mate = side(base, normed_rows.at[mine], normed_rows.at[mine], mate)
    normed_to_far = side(base + 1, normed_rows.at[mine], normed_rows.at[mine], far)
    normed_on = side(base + 2, normed_rows.at[far_rows], normed_rows.at[far_rows], mate)
    pair_sum = side(base + 3, pair_src.at[0], pair_in.at[0], mate)
    far_sum = side(base + 5, far_src, far_in, far)
    grad_on = side(base + 6, sect_src.at[0], sect_in.at[0], next_same)
    wide = feat // PARTS
    cuts = [pl.ds(p * wide, wide) for p in range(PARTS)]
    tail = FRONT + 3 * PIECES
    pair_parts = [
        side(tail + p, pair_src.at[1, :, :, c], pair_in.at[1, :, :, c], mate)
        for p, c in enumerate(cuts)
    ]
    act_parts = [
        [
            side(
                tail + PARTS + 2 * p + n,
                sect_src.at[1 + n, :, c],
                sect_in.at[1 + n, :, c],
                by_way[n],
            )
            for n in (0, 1)
        ]
        for p, c in enumerate(cuts)
    ]

    def total_rows(k, high_of, core_of, cut):
        r = high_of * 2 + core_of
        pieces = []
        for z in range(SIDE):
            own = pl.ds(pl.multiple_of((r * SIDE + z) * BLK, BLK), BLK)
            swap = pl.ds(pl.multiple_of((z * SIDE + r) * BLK, BLK), BLK)
            pieces.append(acc[k, 0, own, cut] + acc[k, 1, swap, cut])
        return jnp.concatenate(pieces, axis=0)

    def pair_part(k, cut):
        for h in (0, 1):
            pair_src[k, h, :, cut] = total_rows(k, h, 1 - core, cut).astype(bf16)

    def chip_rows(k, high_of, cut):
        return total_rows(k, high_of, core, cut) + pair_in[k, high_of, :, cut].astype(f32)

    def grad_pair():
        pair_part(0, slice(None))
        pair_sum.start()

    def norm_stats():
        stat_send(0, 1, stat_total(0, 0))

    def normalize():
        total = unpack(stat_total(0, 1)) / D
        mean_f, mean_b = total[:, 0:1], total[:, 2:3]
        inv_f = lax.rsqrt(total[:, 1:2] - mean_f * mean_f + epsilon)
        inv_b = lax.rsqrt(total[:, 3:4] - mean_b * mean_b + epsilon)
        stats[0] = jnp.broadcast_to(mean_b, (rows, rows))
        stats[1] = jnp.broadcast_to(inv_b, (rows, rows))
        values = xs[plan[0, 1]].astype(f32)
        lhs[1, 0, mine] = ((values - mean_f) * inv_f * gain[...]).astype(bf16)
        normed_to_mate.start()
        normed_to_far.start()

    def normed_forward():
        normed_to_far.wait_recv_into(normed_rows.at[far_rows])
        normed_on.start()

    def normed_done():
        normed_to_mate.wait_recv()
        normed_on.wait_recv()
        for r in (row, mate_row, far_row, far_mate_row):
            swap_rows(1, r)
        for c in (normed_to_mate, normed_to_far, normed_on):
            c.wait_send()

    def grad_far():
        pair_sum.wait_recv()
        own_sum[...] = chip_rows(0, high, slice(None))
        far_src[...] = chip_rows(0, 1 - high, slice(None)).astype(bf16)
        far_sum.start()
        pair_sum.wait_send()

    def hat():
        return (xs[plan[0, 0]].astype(f32) - stats[0, :, 0:1]) * stats[1, :, 0:1]

    def grad_stats():
        far_sum.wait_recv()
        scaled = (own_sum[...] + far_in[...].astype(f32)) * gain[...]
        own_sum[...] = scaled
        stat_send(1, 0, pack([row_sum(scaled), row_sum(scaled * hat())]))
        far_sum.wait_send()

    def grad_stats_more():
        stat_send(1, 1, stat_total(1, 0))

    def grad_out():
        total = unpack(stat_total(1, 1)) / D
        in_grad = grad[0].astype(f32) + stats[1, :, 0:1] * (
            own_sum[...] - total[:, 0:1] - hat() * total[:, 1:2]
        )
        sect_src[0] = in_grad.astype(bf16)
        grad_on.start()

    last = n_pair + len(stages) - 2
    early = (2, 4, 7, 9) if n_pair >= 10 else (1, 2, 4, 5)
    jobs = (
        (early[0], 0, norm_stats),
        (early[1], 0, normalize),
        (early[2], 0, normed_forward),
        (early[3], 0, normed_done),
        (last, 8, grad_pair),
        (last + 1, 3, grad_far),
        (last + 3, 3, grad_stats),
        (last + 4, 0, grad_stats_more),
        (last + 4, 7, grad_out),
    )

    @pl.loop(0, units + len(stages) - 1)
    def _(step):
        for k, stage in enumerate(stages):
            u = step - k

            @pl.when(jnp.logical_and(u >= 0, u < units))
            def _():
                for q in (0, 1):
                    stage(u, q)

            for at, after, job in jobs:
                if after == k:
                    pl.when(step == at)(job)

    for p, c in enumerate(cuts):
        pair_part(1, c)
        pair_parts[p].start()
    for p, c in enumerate(cuts):
        pair_parts[p].wait_recv()
        sect_src[2, :, c] = chip_rows(1, 1 - high, c).astype(bf16)
        act_parts[p][1].start()
        residual = xs[plan[0, 1], :, c].astype(f32) + b_out[:, c]
        sect_src[1, :, c] = (chip_rows(1, high, c) + residual).astype(bf16)
        act_parts[p][0].start()
    grad_on.wait_recv()
    grad_recv[0] = sect_in[0]
    for p, c in enumerate(cuts):
        for n in (0, 1):
            act_parts[p][n].wait_recv()
        act_recv[0, :, c] = (
            sect_in[1, :, c].astype(f32) + sect_in[2, :, c].astype(f32)
        ).astype(bf16)
    for c in pair_parts + act_parts[0] + act_parts[1] + act_parts[2] + [grad_on]:
        c.wait_send()


def store_kernel(*refs):
    n = (len(refs) - 2) // 3
    ins, outs, held = refs[:n], refs[n : 2 * n], refs[2 * n : 3 * n]
    get = [pltpu.make_async_copy(ins[i], held[i], refs[-2].at[i]) for i in range(n)]
    put = [pltpu.make_async_copy(held[i], outs[i], refs[-1].at[i]) for i in range(n)]
    for c in get:
        c.start()
    for i in range(n):
        get[i].wait()
        put[i].start()
    for c in put:
        c.wait()


def body(stash_inputs, stash_hidden, grad_in, w_in, b_in, w_out, b_out, ln_gain, plan, ft=FT):
    _, feat, hid = w_in.shape
    slots = stash_inputs.shape[1]
    tiles = hid // ft
    rows, mine = SIDE * SIDE * BLK, SIDE * BLK
    bf16, f32 = jnp.bfloat16, jnp.float32
    vmem, anyw = pl.BlockSpec(memory_space=pltpu.VMEM), pl.BlockSpec(memory_space=pl.ANY)
    results = pl.pallas_call(
        step_kernel,
        out_shape=(
            jax.ShapeDtypeStruct((1, mine, feat), bf16),
            jax.ShapeDtypeStruct((1, mine, feat), bf16),
            jax.ShapeDtypeStruct((1, BLK, hid), bf16),
        ),
        in_specs=[pl.BlockSpec(memory_space=pltpu.SMEM), vmem, vmem, vmem, vmem] + [anyw] * 4,
        out_specs=(vmem, vmem, vmem),
        scratch_shapes=[
            pltpu.VMEM((2, 2, rows, feat), bf16),
            pltpu.VMEM((slots, mine, feat), bf16),
            pltpu.VMEM((slots, BLK, hid), bf16),
            pltpu.VMEM((2, 2, 8, mine), f32),
            pltpu.VMEM((2, 2, 3, 8, mine), f32),
            pltpu.VMEM((2, mine, mine), f32),
            pltpu.VMEM((2, 2, mine, feat), bf16),
            pltpu.VMEM((2, 2, mine, feat), bf16),
            pltpu.VMEM((PIECES, mine // PIECES, feat), bf16),
            pltpu.VMEM((mine, feat), f32),
            pltpu.VMEM((mine, feat), bf16),
            pltpu.VMEM((mine, feat), bf16),
            pltpu.VMEM((3, mine, feat), bf16),
            pltpu.VMEM((3, mine, feat), bf16),
            pltpu.VMEM((tiles, feat, ft), bf16),
            pltpu.VMEM((tiles, ft, feat), bf16),
            pltpu.VMEM((2, LOCAL, rows, ft), bf16),
            pltpu.VMEM((2, SLOTS, 2, 2 * BLK, ft), bf16),
            pltpu.VMEM((2, SLOTS, 2, 4 * BLK, ft), bf16),
            pltpu.VMEM((2, LOCAL, 4 * BLK, ft), bf16),
            pltpu.VMEM((2, SLOTS, 2, BLK // 2, ft), bf16),
            pltpu.VMEM((2, SLOTS, 2, BLK, ft), bf16),
            pltpu.VMEM((2, SLOTS, SIDE, SIDE, BLK, ft), bf16),
            pltpu.VMEM((2, 2, rows, feat), f32),
            pltpu.SemaphoreType.DMA((4, 2, LOCAL)),
            pltpu.SemaphoreType.DMA((8, 2, SLOTS)),
            pltpu.SemaphoreType.DMA((tiles,)),
            pltpu.SemaphoreType.DMA((tiles,)),
            pltpu.SemaphoreType.DMA((2,)),
            pltpu.SemaphoreType.DMA((FRONT + 3 * PIECES + 3 * PARTS,)),
            pltpu.SemaphoreType.DMA((FRONT + 3 * PIECES + 3 * PARTS,)),
        ],
        compiler_params=pltpu.CompilerParams(
            collective_id=0, has_side_effects=True, vmem_limit_bytes=67043328
        ),
        name="section_step",
    )(plan, grad_in, ln_gain, b_in, b_out, stash_inputs, stash_hidden, w_in, w_out)
    return pl.pallas_call(
        store_kernel,
        out_shape=tuple(jax.ShapeDtypeStruct(r.shape, r.dtype) for r in results),
        in_specs=[anyw] * 3,
        out_specs=(anyw,) * 3,
        scratch_shapes=[pltpu.VMEM(r.shape, r.dtype) for r in results]
        + [pltpu.SemaphoreType.DMA((3,))] * 2,
        compiler_params=pltpu.CompilerParams(vmem_limit_bytes=67043328),
        name="store",
    )(*results)


def solution(mesh):
    in_specs = (
        P("section", None, "row", "col"),
        P("section", None, "col", "row"),
        P("section", "row", "col"),
        P("section", "col", "row"),
        P("section", "row"),
        P("section", "row", "col"),
        P("section", "col"),
        P("section", "col"),
        P("section", None),
    )
    out_specs = (P("section", "row", "col"), P("section", "row", "col"), P("section", "col", "row"))
    return jax.shard_map(body, mesh=mesh, in_specs=in_specs, out_specs=out_specs, check_vma=False)
```

time: 177 us -> 163 us (0.921)
  Pallas kernels: 171 us -> 162 us
  local copies, waits for them, and re-layouts: 5 us -> 0 us
    pallas_call x1, Pallas kernels: 171 us -> 160 us  [body(): pl.pallas_call(step_kernel, out_shape=(jax.ShapeDtypeStruct((1, mine, fea...]
    unnamed x3 -> x0, local copies, waits for them, and re-layouts: 5 us -> none
    pallas_call x0 -> x1, Pallas kernels: none -> 1.99 us  [body(): pl.pallas_call(store_kernel, out_shape=tuple((jax.ShapeDtypeStruct(r.shap...]
where the time goes in v3:
time: 163 us
  Pallas kernels  162 us (99%)
    pallas_call x1, Pallas kernels, body(): pl.pallas_call(step_kernel, out_shape=(jax.ShapeDtypeStruct((1, mine, fea...  160 us

profile of v3, /device:TPU:1, one launch (start us, length us, event | category | flops | bytes accessed | tf_op | source)
XLA Modules:
  0.0 163.1 jit_solution(12479557992698932196)
XLA Ops:
  0.6 160.5 %section_step.1 = (bf16[1,128,768]{2,1,0:T(8,128)(2,1)}, bf16[1,128,768]{2,1,0:T(8,128)(2,1)}, bf16[1,32,6144]{2,1,0:T(8,128)(2,1)}) custom-call(s32[1,2]{1,0:T(1,128)} %plan.1, bf16[1,128,768]{2,1,0:T(8,128)(2,1)} %grad.1, f32[1,768]{1,0:T(1,128)} %gain.1, f32[1,6144]{1,0:T(1,128)} %b_in.1, f32[1,768]{1,0:T(1,128)} %b_out.1, ...), custom_call_target="tpu_custom_call" | custom-call | tf_op jit(solution)/shard_map/section_step/pallas_call | solution.py:663
  161.1 2.0 %store.1 = (bf16[1,128,768]{2,1,0:T(8,128)(2,1)}, bf16[1,128,768]{2,1,0:T(8,128)(2,1)}, bf16[1,32,6144]{2,1,0:T(8,128)(2,1)}) custom-call(bf16[1,128,768]{2,1,0:T(8,128)(2,1)} %get-tuple-element.6.refs_0_, bf16[1,128,768]{2,1,0:T(8,128)(2,1)} %get-tuple-element.7.refs_1_, bf16[1,32,6144]{2,1,0:T(8,128)(2,1)} %get-tuple-element.8.refs_2_), custom_call_target="tpu_custom_call" | custom-call | tf_op jit(solution)/shard_map/store/pallas_call | solution.py:710

commit v4 on v3

--- a/solution.py
+++ b/solution.py
@@ -12,7 +12,7 @@
 LOCAL = 4
 BLK = 32
 LATE_STAGE = 8
-PIECES = 8
+PIECES = 4
 PARTS = 3
 FRONT = 32
 
@@ -76,10 +76,10 @@
 
 def step_kernel(
     plan,
-    grad,
-    gain,
-    b_in,
-    b_out,
+    grad_h,
+    gain_h,
+    b_in_h,
+    b_out_h,
     stash_x,
     stash_h,
     w_in,
@@ -87,6 +87,10 @@
     act_recv,
     grad_recv,
     saved,
+    grad,
+    gain,
+    b_in,
+    b_out,
     lhs,
     xs,
     stash,
@@ -166,26 +170,38 @@
     def side(i, src, dst, dev):
         return Copy(src, dst, side_send.at[i], side_recv.at[i], dev)
 
+    barrier = pltpu.get_barrier_semaphore()
+    for dev in everyone:
+        pl.semaphore_signal(barrier, inc=1, device_id=dev, device_id_type=pl.DeviceIdType.MESH)
+
     loads = [
-        pltpu.make_async_copy(stash_x.at[0], xs, load_sem.at[0]),
-        pltpu.make_async_copy(stash_h.at[0], stash, load_sem.at[1]),
+        pltpu.make_async_copy(src, dst, load_sem.at[i])
+        for i, (src, dst) in enumerate(
+            (
+                (grad_h, grad),
+                (stash_x.at[0], xs),
+                (gain_h, gain),
+                (b_in_h, b_in),
+                (b_out_h, b_out),
+                (stash_h.at[0], stash),
+            )
+        )
     ]
-    loads[0].start()
+    for c in loads[:-1]:
+        c.start()
 
     @pl.loop(0, 2 * n_pair)
     def _(t):
         wout_copy(t).start()
 
-    loads[1].start()
+    loads[-1].start()
 
     @pl.loop(0, 2 * n_pair)
     def _(t):
         win_copy(t).start()
 
-    barrier = pltpu.get_barrier_semaphore()
-    for dev in everyone:
-        pl.semaphore_signal(barrier, inc=1, device_id=dev, device_id_type=pl.DeviceIdType.MESH)
     pl.semaphore_wait(barrier, len(everyone))
+    loads[0].wait()
 
     def row_block(high_of, core_of):
         return pl.ds(pl.multiple_of((high_of * 2 + core_of) * rows, rows), rows)
@@ -264,22 +280,18 @@
     def row_sum(v):
         return jnp.sum(v, axis=1, keepdims=True)
 
-    loads[0].wait()
-    fwd_input = xs[plan[0, 1]].astype(f32)
-    bwd_input = xs[plan[0, 0]].astype(f32)
-    stat_send(
-        0,
-        0,
-        pack(
-            [
-                row_sum(fwd_input),
-                row_sum(fwd_input * fwd_input),
-                row_sum(bwd_input),
-                row_sum(bwd_input * bwd_input),
-            ]
-        ),
-    )
-    loads[1].wait()
+    def first_stats():
+        for c in loads[1:-1]:
+            c.wait()
+        fwd_input = xs[plan[0, 1]].astype(f32)
+        bwd_input = xs[plan[0, 0]].astype(f32)
+        sums = [
+            row_sum(fwd_input),
+            row_sum(fwd_input * fwd_input),
+            row_sum(bwd_input),
+            row_sum(bwd_input * bwd_input),
+        ]
+        stat_send(0, 0, pack(sums))
 
     def swap_rows(k, r):
         for z in range(SIDE):
@@ -290,17 +302,19 @@
     far_row = (1 - high) * 2 + core
     mate_row, far_mate_row = high * 2 + 1 - core, (1 - high) * 2 + 1 - core
     swap_rows(0, row)
+    to_mate.wait_recv()
+    swap_rows(0, mate_row)
     for n in range(PIECES):
         on_hops[n].wait_recv_into(grads.at[piece_of(1 - high, n)])
         far_to_mate[n].start()
-    to_mate.wait_recv()
-    swap_rows(0, mate_row)
     swap_rows(0, far_row)
     for n in range(PIECES):
         far_to_mate[n].wait_recv()
     swap_rows(0, far_mate_row)
-    for c in out_hops + on_hops + far_to_mate + [to_mate]:
-        c.wait_send()
+
+    def front_sent():
+        for c in out_hops + on_hops + far_to_mate + [to_mate]:
+            c.wait_send()
 
     def ring(q, phase):
         axis = (q + phase) % 2
@@ -592,6 +606,9 @@
     last = n_pair + len(stages) - 2
     early = (2, 4, 7, 9) if n_pair >= 10 else (1, 2, 4, 5)
     jobs = (
+        (0, 0, first_stats),
+        (1, 0, front_sent),
+        (3, 3, loads[-1].wait),
         (early[0], 0, norm_stats),
         (early[1], 0, normalize),
         (early[2], 0, normed_forward),
@@ -640,16 +657,13 @@
 
 
 def store_kernel(*refs):
-    n = (len(refs) - 2) // 3
-    ins, outs, held = refs[:n], refs[n : 2 * n], refs[2 * n : 3 * n]
-    get = [pltpu.make_async_copy(ins[i], held[i], refs[-2].at[i]) for i in range(n)]
-    put = [pltpu.make_async_copy(held[i], outs[i], refs[-1].at[i]) for i in range(n)]
-    for c in get:
+    n = len(refs) // 2
+    copies = [
+        pltpu.make_async_copy(refs[i], refs[n + i], refs[-1].at[i]) for i in range(n)
+    ]
+    for c in copies:
         c.start()
-    for i in range(n):
-        get[i].wait()
-        put[i].start()
-    for c in put:
+    for c in copies:
         c.wait()
 
 
@@ -663,13 +677,14 @@
     results = pl.pallas_call(
         step_kernel,
         out_shape=(
-            jax.ShapeDtypeStruct((1, mine, feat), bf16),
-            jax.ShapeDtypeStruct((1, mine, feat), bf16),
-            jax.ShapeDtypeStruct((1, BLK, hid), bf16),
+            pltpu.VMEM((1, mine, feat), bf16),
+            pltpu.VMEM((1, mine, feat), bf16),
+            pltpu.VMEM((1, BLK, hid), bf16),
         ),
-        in_specs=[pl.BlockSpec(memory_space=pltpu.SMEM), vmem, vmem, vmem, vmem] + [anyw] * 4,
+        in_specs=[pl.BlockSpec(memory_space=pltpu.SMEM)] + [anyw] * 8,
         out_specs=(vmem, vmem, vmem),
         scratch_shapes=[
+            *(pltpu.VMEM(v.shape, v.dtype) for v in (grad_in, ln_gain, b_in, b_out)),
             pltpu.VMEM((2, 2, rows, feat), bf16),
             pltpu.VMEM((slots, mine, feat), bf16),
             pltpu.VMEM((slots, BLK, hid), bf16),
@@ -698,23 +713,22 @@
             pltpu.SemaphoreType.DMA((8, 2, SLOTS)),
             pltpu.SemaphoreType.DMA((tiles,)),
             pltpu.SemaphoreType.DMA((tiles,)),
-            pltpu.SemaphoreType.DMA((2,)),
+            pltpu.SemaphoreType.DMA((6,)),
             pltpu.SemaphoreType.DMA((FRONT + 3 * PIECES + 3 * PARTS,)),
             pltpu.SemaphoreType.DMA((FRONT + 3 * PIECES + 3 * PARTS,)),
         ],
         compiler_params=pltpu.CompilerParams(
-            collective_id=0, has_side_effects=True, vmem_limit_bytes=67043328
+            collective_id=0, has_side_effects=True, vmem_limit_bytes=60 << 20
         ),
         name="section_step",
     )(plan, grad_in, ln_gain, b_in, b_out, stash_inputs, stash_hidden, w_in, w_out)
     return pl.pallas_call(
         store_kernel,
         out_shape=tuple(jax.ShapeDtypeStruct(r.shape, r.dtype) for r in results),
-        in_specs=[anyw] * 3,
+        in_specs=[vmem] * 3,
         out_specs=(anyw,) * 3,
-        scratch_shapes=[pltpu.VMEM(r.shape, r.dtype) for r in results]
-        + [pltpu.SemaphoreType.DMA((3,))] * 2,
-        compiler_params=pltpu.CompilerParams(vmem_limit_bytes=67043328),
+        scratch_shapes=[pltpu.SemaphoreType.DMA((3,))],
+        compiler_params=pltpu.CompilerParams(vmem_limit_bytes=4 << 20),
         name="store",
     )(*results)
 

time: 163 us -> 161 us (0.988)
  Pallas kernels: 162 us -> 160 us
where the time goes in v4:
time: 161 us
  Pallas kernels  160 us (99%)
    pallas_call x1, Pallas kernels, body(): pl.pallas_call(step_kernel, out_shape=(pltpu.VMEM((1, mine, feat), bf16),...  159 us

profile of v4, /device:TPU:1, one launch (start us, length us, event | category | flops | bytes accessed | tf_op | source)
XLA Modules:
  0.0 160.8 jit_solution(9664790868095847520)
XLA Ops:
  0.6 159.2 %section_step.1 = (bf16[1,128,768]{2,1,0:T(8,128)(2,1)S(1)}, bf16[1,128,768]{2,1,0:T(8,128)(2,1)S(1)}, bf16[1,32,6144]{2,1,0:T(8,128)(2,1)S(1)}) custom-call(s32[1,2]{1,0:T(1,128)} %plan.1, bf16[1,128,768]{2,1,0:T(8,128)(2,1)} %grad_h.1, f32[1,768]{1,0:T(1,128)} %gain_h.1, f32[1,6144]{1,0:T(1,128)} %b_in_h.1, f32[1,768]{1,0:T(1,128)} %b_out_h.1, ...), custom_call_target="tpu_custom_call" | custom-call | tf_op jit(solution)/shard_map/section_step/pallas_call | solution.py:677
  159.9 0.9 store.1

commit v5 on v4

--- a/solution.py
+++ b/solution.py
@@ -13,7 +13,6 @@
 BLK = 32
 LATE_STAGE = 8
 PIECES = 4
-PARTS = 3
 FRONT = 32
 
 epsilon = 1e-05
@@ -508,44 +507,63 @@
     pair_sum = side(base + 3, pair_src.at[0], pair_in.at[0], mate)
     far_sum = side(base + 5, far_src, far_in, far)
     grad_on = side(base + 6, sect_src.at[0], sect_in.at[0], next_same)
-    wide = feat // PARTS
-    cuts = [pl.ds(p * wide, wide) for p in range(PARTS)]
     tail = FRONT + 3 * PIECES
+    x_far = places[0][2]
+    turns = tuple(places[1][i] for i in (0, 1, 3, 2))
+    soon, late = pl.ds(0, 3 * BLK), pl.ds(3 * BLK, BLK)
+    highs = (high, 1 - high)
     pair_parts = [
-        side(tail + p, pair_src.at[1, :, :, c], pair_in.at[1, :, :, c], mate)
-        for p, c in enumerate(cuts)
+        [
+            side(tail + 2 * n + i, pair_src.at[1, n, r], pair_in.at[1, n, r], mate)
+            for i, r in enumerate((soon, late))
+        ]
+        for n in (0, 1)
     ]
     act_parts = [
         [
-            side(
-                tail + PARTS + 2 * p + n,
-                sect_src.at[1 + n, :, c],
-                sect_in.at[1 + n, :, c],
-                by_way[n],
-            )
-            for n in (0, 1)
+            side(tail + 4 + 2 * n + i, sect_src.at[1 + n, r], sect_in.at[1 + n, r], by_way[n])
+            for i, r in enumerate((soon, late))
         ]
-        for p, c in enumerate(cuts)
+        for n in (0, 1)
     ]
 
-    def total_rows(k, high_of, core_of, cut):
+    def token_rows(k, r, z):
+        own = pl.ds(pl.multiple_of((r * SIDE + z) * BLK, BLK), BLK)
+        swap = pl.ds(pl.multiple_of((z * SIDE + r) * BLK, BLK), BLK)
+        return acc[k, 0, own] + acc[k, 1, swap]
+
+    def total_rows(k, high_of, core_of):
         r = high_of * 2 + core_of
-        pieces = []
-        for z in range(SIDE):
-            own = pl.ds(pl.multiple_of((r * SIDE + z) * BLK, BLK), BLK)
-            swap = pl.ds(pl.multiple_of((z * SIDE + r) * BLK, BLK), BLK)
-            pieces.append(acc[k, 0, own, cut] + acc[k, 1, swap, cut])
-        return jnp.concatenate(pieces, axis=0)
-
-    def pair_part(k, cut):
+        return jnp.concatenate([token_rows(k, r, z) for z in range(SIDE)], axis=0)
+
+    def chip_rows(k, high_of):
+        return total_rows(k, high_of, core) + pair_in[k, high_of].astype(f32)
+
+    def act_pair(n, i):
+        for j in ((0, 1, 2), (3,))[i]:
+            rows = token_rows(1, highs[n] * 2 + 1 - core, turns[j])
+            pair_src[1, n, pl.ds(j * BLK, BLK)] = rows.astype(bf16)
+        pair_parts[n][i].start()
+
+    def act_out(n, i):
+        pair_parts[n][i].wait_recv()
+        for j in ((0, 1, 2), (3,))[i]:
+            at = pl.ds(j * BLK, BLK)
+            rows = token_rows(1, highs[n] * 2 + core, turns[j]) + pair_in[1, n, at].astype(f32)
+            if n == 0:
+                own = pl.ds(pl.multiple_of(turns[j] * BLK, BLK), BLK)
+                rows = rows + (xs[plan[0, 1], own].astype(f32) + b_out[...])
+            sect_src[1 + n, at] = rows.astype(bf16)
+        act_parts[n][i].start()
+
+    def each_soon(core_of, far_ones, job):
+        for n in (0, 1):
+            is_far = highs[n] * 2 + core_of == x_far
+            pl.when(is_far if far_ones else jnp.logical_not(is_far))(lambda n=n: job(n, 0))
+
+    def grad_pair():
         for h in (0, 1):
-            pair_src[k, h, :, cut] = total_rows(k, h, 1 - core, cut).astype(bf16)
-
-    def chip_rows(k, high_of, cut):
-        return total_rows(k, high_of, core, cut) + pair_in[k, high_of, :, cut].astype(f32)
-
-    def grad_pair():
-        pair_part(0, slice(None))
+            pair_src[0, h] = total_rows(0, h, 1 - core).astype(bf16)
         pair_sum.start()
 
     def norm_stats():
@@ -577,8 +595,8 @@
 
     def grad_far():
         pair_sum.wait_recv()
-        own_sum[...] = chip_rows(0, high, slice(None))
-        far_src[...] = chip_rows(0, 1 - high, slice(None)).astype(bf16)
+        own_sum[...] = chip_rows(0, high)
+        far_src[...] = chip_rows(0, 1 - high).astype(bf16)
         far_sum.start()
         pair_sum.wait_send()
 
@@ -618,6 +636,8 @@
         (last + 3, 3, grad_stats),
         (last + 4, 0, grad_stats_more),
         (last + 4, 7, grad_out),
+        (units + 6, 8, lambda: each_soon(1 - core, False, act_pair)),
+        (units + 7, 7, lambda: each_soon(core, False, act_out)),
     )
 
     @pl.loop(0, units + len(stages) - 1)
@@ -634,25 +654,22 @@
                 if after == k:
                     pl.when(step == at)(job)
 
-    for p, c in enumerate(cuts):
-        pair_part(1, c)
-        pair_parts[p].start()
-    for p, c in enumerate(cuts):
-        pair_parts[p].wait_recv()
-        sect_src[2, :, c] = chip_rows(1, 1 - high, c).astype(bf16)
-        act_parts[p][1].start()
-        residual = xs[plan[0, 1], :, c].astype(f32) + b_out[:, c]
-        sect_src[1, :, c] = (chip_rows(1, high, c) + residual).astype(bf16)
-        act_parts[p][0].start()
+    each_soon(1 - core, True, act_pair)
+    for n in (0, 1):
+        act_pair(n, 1)
+    each_soon(core, True, act_out)
+    for n in (0, 1):
+        act_out(n, 1)
     grad_on.wait_recv()
     grad_recv[0] = sect_in[0]
-    for p, c in enumerate(cuts):
+    for i in (0, 1):
         for n in (0, 1):
-            act_parts[p][n].wait_recv()
-        act_recv[0, :, c] = (
-            sect_in[1, :, c].astype(f32) + sect_in[2, :, c].astype(f32)
-        ).astype(bf16)
-    for c in pair_parts + act_parts[0] + act_parts[1] + act_parts[2] + [grad_on]:
+            act_parts[n][i].wait_recv()
+        for j in ((0, 1, 2), (3,))[i]:
+            at = pl.ds(j * BLK, BLK)
+            own = pl.ds(pl.multiple_of(turns[j] * BLK, BLK), BLK)
+            act_recv[0, own] = (sect_in[1, at].astype(f32) + sect_in[2, at].astype(f32)).astype(bf16)
+    for c in sum(pair_parts + act_parts, []) + [grad_on]:
         c.wait_send()
 
 
@@ -714,8 +731,8 @@
             pltpu.SemaphoreType.DMA((tiles,)),
             pltpu.SemaphoreType.DMA((tiles,)),
             pltpu.SemaphoreType.DMA((6,)),
-            pltpu.SemaphoreType.DMA((FRONT + 3 * PIECES + 3 * PARTS,)),
-            pltpu.SemaphoreType.DMA((FRONT + 3 * PIECES + 3 * PARTS,)),
+            pltpu.SemaphoreType.DMA((FRONT + 3 * PIECES + 8,)),
+            pltpu.SemaphoreType.DMA((FRONT + 3 * PIECES + 8,)),
         ],
         compiler_params=pltpu.CompilerParams(
             collective_id=0, has_side_effects=True, vmem_limit_bytes=60 << 20

time: 161 us -> 158 us (0.981)
  Pallas kernels: 160 us -> 157 us
    pallas_call x1, Pallas kernels: 159 us -> 156 us  [body(): pl.pallas_call(step_kernel, out_shape=(pltpu.VMEM((1, mine, feat), bf16),...]
where the time goes in v5:
time: 158 us
  Pallas kernels  157 us (99%)
    pallas_call x1, Pallas kernels, body(): pl.pallas_call(step_kernel, out_shape=(pltpu.VMEM((1, mine, feat), bf16),...  156 us

profile of v5, /device:TPU:1, one launch (start us, length us, event | category | flops | bytes accessed | tf_op | source)
XLA Modules:
  0.0 157.7 jit_solution(14951948718127200642)
XLA Ops:
  0.6 156.2 %section_step.1 = (bf16[1,128,768]{2,1,0:T(8,128)(2,1)S(1)}, bf16[1,128,768]{2,1,0:T(8,128)(2,1)S(1)}, bf16[1,32,6144]{2,1,0:T(8,128)(2,1)S(1)}) custom-call(s32[1,2]{1,0:T(1,128)} %plan.1, bf16[1,128,768]{2,1,0:T(8,128)(2,1)} %grad_h.1, f32[1,768]{1,0:T(1,128)} %gain_h.1, f32[1,6144]{1,0:T(1,128)} %b_in_h.1, f32[1,768]{1,0:T(1,128)} %b_out_h.1, ...), custom_call_target="tpu_custom_call" | custom-call | tf_op jit(solution)/shard_map/section_step/pallas_call | solution.py:694
  156.8 0.9 store.1

commit v6 on v5

--- a/solution.py
+++ b/solution.py
@@ -622,14 +622,14 @@
         grad_on.start()
 
     last = n_pair + len(stages) - 2
-    early = (2, 4, 7, 9) if n_pair >= 10 else (1, 2, 4, 5)
+    early = (2, 4, 7, 9) if n_pair >= 10 else (2, 3, 4, 5)
     jobs = (
-        (0, 0, first_stats),
+        (1, 1, first_stats),
         (1, 0, front_sent),
         (3, 3, loads[-1].wait),
         (early[0], 0, norm_stats),
         (early[1], 0, normalize),
-        (early[2], 0, normed_forward),
+        (early[2], 4, normed_forward),
         (early[3], 0, normed_done),
         (last, 8, grad_pair),
         (last + 1, 3, grad_far),

time: 158 us -> 158 us (level)
  no operation moved by 1% of the time
where the time goes in v6:
time: 158 us
  Pallas kernels  157 us (99%)
    pallas_call x1, Pallas kernels, body(): pl.pallas_call(step_kernel, out_shape=(pltpu.VMEM((1, mine, feat), bf16),...  156 us

profile of v6, /device:TPU:1, one launch (start us, length us, event | category | flops | bytes accessed | tf_op | source)
XLA Modules:
  0.0 157.7 jit_solution(12994922085669388992)
XLA Ops:
  0.6 156.2 %section_step.1 = (bf16[1,128,768]{2,1,0:T(8,128)(2,1)S(1)}, bf16[1,128,768]{2,1,0:T(8,128)(2,1)S(1)}, bf16[1,32,6144]{2,1,0:T(8,128)(2,1)S(1)}) custom-call(s32[1,2]{1,0:T(1,128)} %plan.1, bf16[1,128,768]{2,1,0:T(8,128)(2,1)} %grad_h.1, f32[1,768]{1,0:T(1,128)} %gain_h.1, f32[1,6144]{1,0:T(1,128)} %b_in_h.1, f32[1,768]{1,0:T(1,128)} %b_out_h.1, ...), custom_call_target="tpu_custom_call" | custom-call | tf_op jit(solution)/shard_map/section_step/pallas_call | solution.py:694
  156.8 0.9 store.1
